TPU v7x, 128 devices: a whole 4x4x4 slice. The times are simulated.
128 devices in a mesh: band: 8 (over x, y_lo), ga: 16 (over z, y_hi, core).
Axes of the slice: x: 4, y: 4 (y_hi: 2, y_lo: 2; y = y_hi * 2 + y_lo), z: 4, core: 2. Of those that a mesh axis runs over, the one named last changes fastest.
Arguments:
- psi: float32 [4096, 8192], P('band', 'ga'), may hold values from -6 to 6
- lower: float32 [4096, 4096], P('band', 'ga'), as said below
Outputs:
- orthonormal: float32 [4096, 8192], P('band', 'ga')
- block_intersection: float32 [4096, 512], P('band')
Inputs may be any that keep to these rules, and one draw needn't show every extreme that they name: lower is lower triangular with its diagonal between 1 and 2.
All inputs are finite; a program needn't handle non-finite values.
Results may differ from a plain program's by a relative error of at most 0.00022.
Values sent between devices are 32-bit elements; how exact they have to be, the bound alone decides.
A program may use at most 64 MiB of HBM per device.

v0:
```python
import jax
import jax.numpy as jnp
from jax import lax
from jax.sharding import PartitionSpec as P


def padded_to(lines, length):
    spare = -lines.shape[0] % length
    if not spare:
        return lines
    return jnp.concatenate([lines, jnp.zeros((spare, *lines.shape[1:]), lines.dtype)])


def broadcast_by_parts(array, axis, root):
    lines = jnp.where(lax.axis_index(axis) == root, array, jnp.zeros_like(array)).reshape(
        -1, *array.shape[1:][-1:]
    )
    padded = padded_to(lines, lax.axis_size(axis))
    own = lax.psum_scatter(padded, axis, scatter_dimension=0, tiled=True)
    return lax.all_gather(own, axis, axis=0, tiled=True)[: len(lines)].reshape(array.shape)


def sum_in_two_steps(array, axis):
    lines = array.reshape(-1, *array.shape[1:][-1:])
    own = lax.psum_scatter(
        padded_to(lines, lax.axis_size(axis)), axis, scatter_dimension=0, tiled=True
    )
    whole = lax.all_gather(own, axis).reshape(-1, *lines.shape[1:])
    return lax.slice_in_dim(whole, 0, len(lines)).reshape(array.shape)


def local(psi, lower):
    myblock = lax.axis_index("band")
    sections = lax.axis_size("band")
    nrows = psi.shape[0]
    width = psi.shape[1]
    full_rows = lax.all_gather(lower, "ga", axis=1, tiled=True)
    own_tile = lax.dynamic_slice_in_dim(full_rows, myblock * nrows, nrows, 1)

    def finish(rhs):
        return jax.scipy.linalg.solve_triangular(own_tile, rhs, lower=True)

    def nothing(rhs):
        return jnp.zeros_like(rhs)

    pieces = 1
    span = width // pieces

    def section(section_idx, carry):
        totals, results = carry
        tile = lax.dynamic_slice_in_dim(full_rows, section_idx * nrows, nrows, 1)
        rhs = psi - totals[0]
        ready = lax.cond(myblock == section_idx, finish, nothing, rhs)
        arrived = broadcast_by_parts(ready, "band", section_idx)
        new_results = [jnp.where(myblock == section_idx, ready, results[0])]
        term = jnp.dot(
            tile, arrived, precision=lax.Precision.HIGHEST, preferred_element_type=jnp.float32
        )
        new_totals = [jnp.where(section_idx < myblock, totals[0] + term, totals[0])]
        return (tuple(new_totals), tuple(new_results))

    blank = tuple((jnp.zeros((nrows, span), jnp.float32) for piece in range(pieces)))
    totals, results = lax.fori_loop(0, sections, section, (blank, blank))
    solved = results[0]
    local_intersection = jnp.dot(
        solved, solved.T, precision=lax.Precision.HIGHEST, preferred_element_type=jnp.float32
    )
    intersection = sum_in_two_steps(local_intersection, "ga") / (width * lax.axis_size("ga"))
    return (solved, intersection)


def solution(mesh):
    return jax.shard_map(
        local,
        mesh=mesh,
        in_specs=(P("band", "ga"), P("band", "ga")),
        out_specs=(P("band", "ga"), P("band", None)),
        check_vma=False,
    )
```

profile of v0, /device:TPU:15, one launch (start us, length us, event | category | flops | bytes accessed | tf_op | source)
XLA Modules:
  0.0 1326.2 jit_solution(7465436344292886088)
XLA Ops:
  7.9 80.7 %all-gather.5.cloned.1.call-done = f32[512,4096]{1,0:T(8,128)} async-done(((f32[512,256]{1,0:T(8,128)}), f32[512,4096]{1,0:T(8,128)}) %all-gather.5.cloned.1.call-update) | async-done | bytes 8388624 | tf_op jit(solution)/shard_map/all_gather | solution.py:37
  88.7 2.3 constant_dynamic-slice_fusion.1
  90.9 1102.6 %while.18 = (s32[]{:T(128)}, f32[512,512]{1,0:T(8,128)S(1)}, f32[512,512]{1,0:T(8,128)S(1)}, s32[]{:T(128)}, f32[512,4096]{1,0:T(8,128)}, /*index=5*/f32[512,512...) while((s32[]{:T(128)}, f32[512,512]{1,0:T(8,128)S(1)}, ...), condition=%wide.region_4.5_spmd.clone, body=%wide.region_0.4_spmd.clone.sunk | while | flops 2621112320 | bytes 30935096 | solution.py:63
  91.2 1.4 select_select_fusion.2
  92.6 85.0 %reduce-scatter.5.cloned.1.call-done = f32[64,512]{1,0:T(8,128)} async-done(((f32[512,512]{1,0:T(8,128)}), f32[64,512]{1,0:T(8,128)}) %reduce-scatter.5.cloned.1.call-update) | async-done | bytes 131088 | tf_op jit(solution)/shard_map/while/body/eval_jaxpr/reduce_scatter | solution.py:19
  177.7 38.7 %all-gather.9.cloned.1.call-done = f32[512,512]{1,0:T(8,128)} async-done(((f32[64,512]{1,0:T(8,128)}), f32[512,512]{1,0:T(8,128)}) %all-gather.9.cloned.1.call-update) | async-done | bytes 1048592 | tf_op jit(solution)/shard_map/while/body/eval_jaxpr/all_gather | solution.py:20
  216.4 3.4 add_select_fusion.2
  220.1 1.4 select_select_fusion.2
  221.6 93.9 %reduce-scatter.5.cloned.1.call-done = f32[64,512]{1,0:T(8,128)} async-done(((f32[512,512]{1,0:T(8,128)}), f32[64,512]{1,0:T(8,128)}) %reduce-scatter.5.cloned.1.call-update) | async-done | bytes 131088 | tf_op jit(solution)/shard_map/while/body/eval_jaxpr/reduce_scatter | solution.py:19
  315.6 38.9 %all-gather.9.cloned.1.call-done = f32[512,512]{1,0:T(8,128)} async-done(((f32[64,512]{1,0:T(8,128)}), f32[512,512]{1,0:T(8,128)}) %all-gather.9.cloned.1.call-update) | async-done | bytes 1048592 | tf_op jit(solution)/shard_map/while/body/eval_jaxpr/all_gather | solution.py:20
  354.5 3.4 add_select_fusion.2
  358.2 1.4 select_select_fusion.2
  359.7 94.1 %reduce-scatter.5.cloned.1.call-done = f32[64,512]{1,0:T(8,128)} async-done(((f32[512,512]{1,0:T(8,128)}), f32[64,512]{1,0:T(8,128)}) %reduce-scatter.5.cloned.1.call-update) | async-done | bytes 131088 | tf_op jit(solution)/shard_map/while/body/eval_jaxpr/reduce_scatter | solution.py:19
  453.8 39.2 %all-gather.9.cloned.1.call-done = f32[512,512]{1,0:T(8,128)} async-done(((f32[64,512]{1,0:T(8,128)}), f32[512,512]{1,0:T(8,128)}) %all-gather.9.cloned.1.call-update) | async-done | bytes 1048592 | tf_op jit(solution)/shard_map/while/body/eval_jaxpr/all_gather | solution.py:20
  493.0 3.4 add_select_fusion.2
  496.7 1.4 select_select_fusion.2
  498.2 93.5 %reduce-scatter.5.cloned.1.call-done = f32[64,512]{1,0:T(8,128)} async-done(((f32[512,512]{1,0:T(8,128)}), f32[64,512]{1,0:T(8,128)}) %reduce-scatter.5.cloned.1.call-update) | async-done | bytes 131088 | tf_op jit(solution)/shard_map/while/body/eval_jaxpr/reduce_scatter | solution.py:19
  591.7 39.3 %all-gather.9.cloned.1.call-done = f32[512,512]{1,0:T(8,128)} async-done(((f32[64,512]{1,0:T(8,128)}), f32[512,512]{1,0:T(8,128)}) %all-gather.9.cloned.1.call-update) | async-done | bytes 1048592 | tf_op jit(solution)/shard_map/while/body/eval_jaxpr/all_gather | solution.py:20
  631.0 3.4 add_select_fusion.2
  634.7 1.4 select_select_fusion.2
  636.2 95.4 %reduce-scatter.5.cloned.1.call-done = f32[64,512]{1,0:T(8,128)} async-done(((f32[512,512]{1,0:T(8,128)}), f32[64,512]{1,0:T(8,128)}) %reduce-scatter.5.cloned.1.call-update) | async-done | bytes 131088 | tf_op jit(solution)/shard_map/while/body/eval_jaxpr/reduce_scatter | solution.py:19
  731.6 39.1 %all-gather.9.cloned.1.call-done = f32[512,512]{1,0:T(8,128)} async-done(((f32[64,512]{1,0:T(8,128)}), f32[512,512]{1,0:T(8,128)}) %all-gather.9.cloned.1.call-update) | async-done | bytes 1048592 | tf_op jit(solution)/shard_map/while/body/eval_jaxpr/all_gather | solution.py:20
  770.7 3.4 add_select_fusion.2
  774.4 1.4 select_select_fusion.2
  775.9 95.0 %reduce-scatter.5.cloned.1.call-done = f32[64,512]{1,0:T(8,128)} async-done(((f32[512,512]{1,0:T(8,128)}), f32[64,512]{1,0:T(8,128)}) %reduce-scatter.5.cloned.1.call-update) | async-done | bytes 131088 | tf_op jit(solution)/shard_map/while/body/eval_jaxpr/reduce_scatter | solution.py:19
  870.9 39.1 %all-gather.9.cloned.1.call-done = f32[512,512]{1,0:T(8,128)} async-done(((f32[64,512]{1,0:T(8,128)}), f32[512,512]{1,0:T(8,128)}) %all-gather.9.cloned.1.call-update) | async-done | bytes 1048592 | tf_op jit(solution)/shard_map/while/body/eval_jaxpr/all_gather | solution.py:20
  910.0 3.4 add_select_fusion.2
  913.7 1.4 select_select_fusion.2
  915.2 95.9 %reduce-scatter.5.cloned.1.call-done = f32[64,512]{1,0:T(8,128)} async-done(((f32[512,512]{1,0:T(8,128)}), f32[64,512]{1,0:T(8,128)}) %reduce-scatter.5.cloned.1.call-update) | async-done | bytes 131088 | tf_op jit(solution)/shard_map/while/body/eval_jaxpr/reduce_scatter | solution.py:19
  1011.1 39.0 %all-gather.9.cloned.1.call-done = f32[512,512]{1,0:T(8,128)} async-done(((f32[64,512]{1,0:T(8,128)}), f32[512,512]{1,0:T(8,128)}) %all-gather.9.cloned.1.call-update) | async-done | bytes 1048592 | tf_op jit(solution)/shard_map/while/body/eval_jaxpr/all_gather | solution.py:20
  1050.1 3.4 add_select_fusion.2
  1053.7 56.2 %conditional.3 = (f32[512,512]{1,0:T(8,128)S(1)}) conditional(s32[]{:T(128)} %convert_element_type.9, () %tuple.61, (f32[512,512]{1,0:T(8,128)}, f32[512,512]{1,0:T(8,128)}, f32[512,512]{1,0:T(8,128)S(1)}) %tuple.62), branch_computations={%region_1.0_spmd, %region_2.2_spmd} | conditional | flops 1008926720 | bytes 13371097 | solution.py:53
  1053.7 1.3 fusion
  1055.1 10.0 while.17
  1055.7 1.9 bitcast_dynamic-update-slice_fusion.2
  1058.2 1.9 bitcast_dynamic-update-slice_fusion.2
  1060.7 1.9 bitcast_dynamic-update-slice_fusion.2
  1063.2 1.9 bitcast_dynamic-update-slice_fusion.2
  1065.1 40.1 %custom-call.3 = f32[4,128,128]{1,2,0:T(8,128)S(1)} custom-call(f32[4,128,128]{2,1,0:T(8,128)} %get-tuple-element.151), custom_call_target="InvertDiagBlocksLowerTriangular" | custom-call | tf_op jit(solution)/shard_map/while/body/eval_jaxpr/cond/branch_1_fun/jit(_solve_triangular)/triangular_solve | solution.py:41
  1105.2 1.4 sub.7
  1109.9 1.4 select_select_fusion.2
  1111.3 39.6 %reduce-scatter.5.cloned.1.call-done = f32[64,512]{1,0:T(8,128)} async-done(((f32[512,512]{1,0:T(8,128)}), f32[64,512]{1,0:T(8,128)}) %reduce-scatter.5.cloned.1.call-update) | async-done | bytes 131088 | tf_op jit(solution)/shard_map/while/body/eval_jaxpr/reduce_scatter | solution.py:19
  1151.0 39.1 %all-gather.9.cloned.1.call-done = f32[512,512]{1,0:T(8,128)} async-done(((f32[64,512]{1,0:T(8,128)}), f32[512,512]{1,0:T(8,128)}) %all-gather.9.cloned.1.call-update) | async-done | bytes 1048592 | tf_op jit(solution)/shard_map/while/body/eval_jaxpr/all_gather | solution.py:20
  1190.1 3.4 add_select_fusion.2
  1193.5 2.8 fusion.22
  1196.5 72.9 %reduce-scatter.3.cloned.1.call-done = f32[32,512]{1,0:T(8,128)} async-done(((f32[512,512]{1,0:T(8,128)}), f32[32,512]{1,0:T(8,128)}) %reduce-scatter.3.cloned.1.call-update) | async-done | bytes 65552 | tf_op jit(solution)/shard_map/reduce_scatter | solution.py:25
  1269.3 48.1 %all-gather.7.cloned.1.call-done = f32[512,512]{1,0:T(8,128)} async-done(((f32[32,512]{1,0:T(8,128)}), f32[512,512]{1,0:T(8,128)}) %all-gather.7.cloned.1.call-update) | async-done | bytes 1048592 | tf_op jit(solution)/shard_map/all_gather | solution.py:28
  1317.4 2.3 broadcast_multiply_fusion
  (83 shorter events, 9.8 us)
Async XLA Ops:
  7.2 81.5 %all-gather.5.cloned.1.call-start = ((), (), s32[]{:S(2)}) async-start(), calls=%async_computation.2 | async-start | bytes 8912896 | tf_op jit(solution)/shard_map/all_gather | solution.py:37
  90.9 86.8 %reduce-scatter.5.cloned.1.call-start = ((), (), s32[]{:S(2)}) async-start(), calls=%async_computation.5 | async-start | bytes 1179648 | tf_op jit(solution)/shard_map/while/body/eval_jaxpr/reduce_scatter | solution.py:19
  92.6 123.9 %all-gather.9.cloned.1.call-start = ((), (), s32[]{:S(2)}) async-start(), calls=%async_computation.6 | async-start | bytes 1179648 | tf_op jit(solution)/shard_map/while/body/eval_jaxpr/all_gather | solution.py:20
  219.8 95.7 %reduce-scatter.5.cloned.1.call-start = ((), (), s32[]{:S(2)}) async-start(), calls=%async_computation.5 | async-start | bytes 1179648 | tf_op jit(solution)/shard_map/while/body/eval_jaxpr/reduce_scatter | solution.py:19
  221.6 132.9 %all-gather.9.cloned.1.call-start = ((), (), s32[]{:S(2)}) async-start(), calls=%async_computation.6 | async-start | bytes 1179648 | tf_op jit(solution)/shard_map/while/body/eval_jaxpr/all_gather | solution.py:20
  357.9 95.8 %reduce-scatter.5.cloned.1.call-start = ((), (), s32[]{:S(2)}) async-start(), calls=%async_computation.5 | async-start | bytes 1179648 | tf_op jit(solution)/shard_map/while/body/eval_jaxpr/reduce_scatter | solution.py:19
  359.6 133.4 %all-gather.9.cloned.1.call-start = ((), (), s32[]{:S(2)}) async-start(), calls=%async_computation.6 | async-start | bytes 1179648 | tf_op jit(solution)/shard_map/while/body/eval_jaxpr/all_gather | solution.py:20
  496.4 95.3 %reduce-scatter.5.cloned.1.call-start = ((), (), s32[]{:S(2)}) async-start(), calls=%async_computation.5 | async-start | bytes 1179648 | tf_op jit(solution)/shard_map/while/body/eval_jaxpr/reduce_scatter | solution.py:19
  498.1 132.8 %all-gather.9.cloned.1.call-start = ((), (), s32[]{:S(2)}) async-start(), calls=%async_computation.6 | async-start | bytes 1179648 | tf_op jit(solution)/shard_map/while/body/eval_jaxpr/all_gather | solution.py:20
  634.4 97.2 %reduce-scatter.5.cloned.1.call-start = ((), (), s32[]{:S(2)}) async-start(), calls=%async_computation.5 | async-start | bytes 1179648 | tf_op jit(solution)/shard_map/while/body/eval_jaxpr/reduce_scatter | solution.py:19
  636.1 134.6 %all-gather.9.cloned.1.call-start = ((), (), s32[]{:S(2)}) async-start(), calls=%async_computation.6 | async-start | bytes 1179648 | tf_op jit(solution)/shard_map/while/body/eval_jaxpr/all_gather | solution.py:20
  774.1 96.8 %reduce-scatter.5.cloned.1.call-start = ((), (), s32[]{:S(2)}) async-start(), calls=%async_computation.5 | async-start | bytes 1179648 | tf_op jit(solution)/shard_map/while/body/eval_jaxpr/reduce_scatter | solution.py:19
  775.8 134.2 %all-gather.9.cloned.1.call-start = ((), (), s32[]{:S(2)}) async-start(), calls=%async_computation.6 | async-start | bytes 1179648 | tf_op jit(solution)/shard_map/while/body/eval_jaxpr/all_gather | solution.py:20
  913.4 97.7 %reduce-scatter.5.cloned.1.call-start = ((), (), s32[]{:S(2)}) async-start(), calls=%async_computation.5 | async-start | bytes 1179648 | tf_op jit(solution)/shard_map/while/body/eval_jaxpr/reduce_scatter | solution.py:19
  915.2 134.9 %all-gather.9.cloned.1.call-start = ((), (), s32[]{:S(2)}) async-start(), calls=%async_computation.6 | async-start | bytes 1179648 | tf_op jit(solution)/shard_map/while/body/eval_jaxpr/all_gather | solution.py:20
  1053.5 97.4 %reduce-scatter.5.cloned.1.call-start = ((), (), s32[]{:S(2)}) async-start(), calls=%async_computation.5 | async-start | bytes 1179648 | tf_op jit(solution)/shard_map/while/body/eval_jaxpr/reduce_scatter | solution.py:19
  1111.3 78.8 %all-gather.9.cloned.1.call-start = ((), (), s32[]{:S(2)}) async-start(), calls=%async_computation.6 | async-start | bytes 1179648 | tf_op jit(solution)/shard_map/while/body/eval_jaxpr/all_gather | solution.py:20
  1193.5 126.2 %copy-start = (f32[512,512]{1,0:T(8,128)}, f32[512,512]{1,0:T(8,128)S(1)}, u32[]{:S(2)}) copy-start(f32[512,512]{1,0:T(8,128)S(1)} %get-tuple-element.141) | copy-start | bytes 3145732
  1193.5 75.8 %reduce-scatter.3.cloned.1.call-start = ((), (), s32[]{:S(2)}) async-start(), calls=%async_computation.3 | async-start | bytes 1114112 | tf_op jit(solution)/shard_map/reduce_scatter | solution.py:25
  1196.4 121.0 %all-gather.7.cloned.1.call-start = ((), (), s32[]{:S(2)}) async-start(), calls=%async_computation.4 | async-start | bytes 1114112 | tf_op jit(solution)/shard_map/all_gather | solution.py:28
Sparse Core Ops, SparseCore 0:
  10.3 78.2 all-gather.4
  94.7 82.9 reduce-scatter.4
  179.3 37.0 all-gather.8
  223.3 92.1 reduce-scatter.4
  317.0 37.4 all-gather.8
  361.4 92.3 reduce-scatter.4
  455.4 37.5 all-gather.8
  500.2 91.4 reduce-scatter.4
  593.3 37.6 all-gather.8
  637.8 93.6 reduce-scatter.4
  733.2 37.4 all-gather.8
  777.6 93.2 reduce-scatter.4
  872.5 37.4 all-gather.8
  916.9 94.1 reduce-scatter.4
  1012.6 37.4 all-gather.8
  1111.4 39.4 reduce-scatter.4
  1152.4 37.6 all-gather.8
  1198.3 70.9 reduce-scatter.2
  1271.8 45.5 all-gather.6
where the time goes:
time: 1330 us
  waiting for transfers between devices  1210 us (91%)
  other arithmetic  57.2 us (4%)
  matrix products  33 us (2%)
  between operations  13.8 us (1%)
    reduce_scatter x8, waiting for transfers between devices, broadcast_by_parts(): own = lax.psum_scatter(padded, axis, scatter_dimension=0, tiled=True)  692 us
    all_gather x8, waiting for transfers between devices, broadcast_by_parts(): lax.all_gather(own, axis, axis=0, tiled=True)[:len(lines)]  312 us
    all_gather x1, waiting for transfers between devices, local(): full_rows = lax.all_gather(lower, 'ga', axis=1, tiled=True)  80.7 us
    reduce_scatter x1, waiting for transfers between devices, sum_in_two_steps(): lax.psum_scatter(padded_to(lines, lax.axis_size(axis)), axis, scatter_dim...  72.9 us
    all_gather x1, waiting for transfers between devices, sum_in_two_steps(): whole = lax.all_gather(own, axis).reshape(-1, *lines.shape[1:])  48.1 us
    another operation x4, other arithmetic, finish(): return jax.scipy.linalg.solve_triangular(own_tile, rhs, lower=True)  41.5 us
    dot_general x8, matrix products, section(): jnp.dot(tile, arrived, precision=lax.Precision.HIGHEST, preferred_element...  27.1 us
  transfers between devices with their start and end apart: 19, of which 19 were waited for; matrix products, arithmetic and copies ran while one was open for 0% of the time, Pallas kernels for 0%

commit v1 on v0

v1 whole, which is shorter than its diff:
```python
import jax
import jax.numpy as jnp
from jax import lax
from jax.experimental import pallas as pl
from jax.experimental.pallas import tpu as pltpu
from jax.sharding import PartitionSpec as P

MESH = pl.DeviceIdType.MESH
F32 = jnp.float32
BF16 = jnp.bfloat16
NG = 8192


def split(a):
    high = a.astype(BF16)
    return high, (a - high.astype(F32)).astype(BF16)


def product(a, b, dims=(((1,), (0,)), ((), ()))):
    ah, al = split(a)
    bh, bl = split(b)

    def dot(p, q):
        return lax.dot_general(p, q, dims, preferred_element_type=F32)

    return dot(ah, bh) + (dot(ah, bl) + dot(al, bh))


def kernel(
    psi, lower, out, inter,
    tiles, ys, rhs, owned, part, half, pieces, whole, inverse,
    tile_sem, ring_sem, cross_sem, pair_sem, swap_sem, rhs_sem, rhs_send,
    y_sem, y_send, own_sem, own_send, half_sem, rs_sem, rs_send, ag_sem, ag_send,
    ag_cross, local_sem,
):
    band = lax.axis_index("band")
    ga = lax.axis_index("ga")
    x, y_lo = band // 2, band % 2
    z, y_hi, c = ga // 4, (ga // 2) % 2, ga % 2
    y = 2 * y_hi + y_lo
    h_own = x // 2
    outer = jnp.logical_or(x == 0, x == 3)
    x_low = jnp.minimum(x, 3 - x)
    place = 2 * h_own + y_lo

    def device(dx, dy, dz, dc):
        return (2 * dx + dy % 2, 4 * dz + 2 * (dy // 2) + dc)

    def xs(h):
        return x_low if h == 0 else 3 - x_low

    def slot(row, j, a, b):
        return ((row * 8 + j) * 2 + a) * 2 + b

    pending = []

    def send(cond, src, dst, s_sem, r_sem, target, later=True):
        copy = pltpu.make_async_remote_copy(
            src_ref=src, dst_ref=dst, send_sem=s_sem, recv_sem=r_sem,
            device_id=target, device_id_type=MESH,
        )
        if cond is None:
            copy.start()
        else:
            pl.when(cond)(copy.start)
        if later:
            pending.append((cond, copy))
        return copy

    def arrived(ref, sem):
        pltpu.make_async_copy(ref, ref, sem).wait()

    psi_here = pltpu.make_async_copy(
        psi.at[:, pl.ds(pl.multiple_of(128 * place, 128), 128)], rhs.at[place], local_sem.at[0]
    )
    psi_here.start()

    j_own = 2 * z + y_hi
    loads = []
    for a in range(2):
        load = pltpu.make_async_copy(
            lower.at[256 * a : 256 * a + 256, :], tiles.at[slot(place, j_own, a, c)],
            local_sem.at[1 + a],
        )
        load.start()
        loads.append(load)

    for q in range(4):
        send(
            place != q,
            psi.at[:, 128 * q : 128 * q + 128], rhs.at[place],
            rhs_send.at[q], rhs_sem.at[place],
            device(xs(q // 2), 2 * y_hi + q % 2, z, c),
        )
    for load in loads:
        load.wait()

    @pl.when(j_own == band)
    def _():
        where = slot(place, j_own, c, c)
        rows = lax.broadcasted_iota(jnp.int32, (256, 256), 0)
        cols = lax.broadcasted_iota(jnp.int32, (256, 256), 1)
        tri = tiles[where]
        diag = jnp.where(rows == cols, tri, 0.0)
        down = 1.0 / jnp.sum(diag, axis=1, keepdims=True)
        across = 1.0 / jnp.sum(diag, axis=0, keepdims=True)
        pairs = jnp.logical_and(rows == cols + 1, rows % 2 == 1)
        inverse[...] = jnp.where(rows == cols, down, 0.0) - jnp.where(
            pairs, tri * down * across, 0.0
        )

        def level(k, carry):
            rk, ck = rows >> k, cols >> k
            inside = jnp.logical_and(rk == ck + 1, rk % 2 == 1)
            below = jnp.where(inside, tiles[where], 0.0)
            now = inverse[...]
            inverse[...] = now - product(now, product(below, now))
            return carry

        lax.fori_loop(1, 8, level, 0)
        tiles[where] = inverse[...]

    def place_of(v):
        return lax.rem(v + 8, 4)

    def event(h, a, k, s):
        sgn = 1 - 2 * a
        yo = place_of(y - sgn * (k * c + s * (1 - c)))
        zo = place_of(z - sgn * (k * (1 - c) + s * c))
        row, j = 2 * h + yo % 2, 2 * zo + yo // 2
        i = 2 * xs(h) + yo % 2
        here = slot(row, j, a, c)
        real = 2 * j + c <= 2 * i + a
        ref = tiles.at[here]
        if k or s:
            pl.when(real)(lambda: arrived(ref, tile_sem.at[here]))
        else:
            mine = h_own == h
            pl.when(jnp.logical_and(real, jnp.logical_not(mine)))(
                lambda: arrived(ref, tile_sem.at[here])
            )
        first = device(x, place_of(y + sgn * c), place_of(z + sgn * (1 - c)), c)
        second = device(x, place_of(y + sgn * (1 - c)), place_of(z + sgn * c), c)
        if s == 0 and k < 3:
            send(real, ref, ref, ring_sem.at[(h * 2 + a) * 3 + k], tile_sem.at[here], first)
        if s < 3:
            send(real, ref, ref, cross_sem.at[((h * 2 + a) * 4 + k) * 3 + s],
                 tile_sem.at[here], second)
        send(real, ref, ref, pair_sem.at[((h * 2 + a) * 4 + k) * 4 + s], tile_sem.at[here],
             device(x, y, z, 1 - c))

    for a in range(2):
        here = slot(place, j_own, a, c)
        send(2 * j_own + c <= 2 * band + a, tiles.at[here], tiles.at[here], swap_sem.at[a],
             tile_sem.at[here], device(3 - x, y, z, c))

    def line(h):
        for k in range(4):
            for a in range(2):
                event(h, a, k, 0)

    def across(h, s):
        for k in range(4):
            for a in range(2):
                event(h, a, k, s)

    def tile(row, j, a, b):
        return tiles[slot(row, j, a, b)]

    def from_sibling(row, j, a):
        here = slot(row, j, a, 1 - c)
        arrived(tiles.at[here], tile_sem.at[here])

    def update(row, j):
        for a in range(2):
            from_sibling(row, j, a)
        top, bottom = ys[2 * j], ys[2 * j + 1]
        for a in range(2):
            rhs[row, 256 * a : 256 * a + 256, :] = rhs[row, 256 * a : 256 * a + 256, :] - (
                product(tile(row, j, a, 0), top) + product(tile(row, j, a, 1), bottom)
            )

    def solve(row, i):
        @pl.when(c == 0)
        def _():
            from_sibling(row, i, 1)

        @pl.when(c == 1)
        def _():
            from_sibling(row, i, 0)
            from_sibling(row, i, 1)

        top = product(tile(row, i, 0, 0), rhs[row, 0:256, :])
        ys[2 * i] = top
        bottom = product(
            tile(row, i, 1, 1), rhs[row, 256:512, :] - product(tile(row, i, 1, 0), top)
        )
        ys[2 * i + 1] = bottom

    def deliver(h, r, later):
        row = 2 * h + r
        i = 2 * xs(h) + r
        block = ys.at[pl.ds(2 * i, 2)]
        send(None if h == 0 else jnp.logical_not(outer), block, block, y_send.at[row],
             y_sem.at[i], device(x + 1 - 2 * (x % 2), y, z, c), later)
        send(place != row, block, owned.at[place], own_send.at[row], own_sem.at[place],
             device(xs(h), 2 * y_hi + r, z, c), later)

    def stage(h, later):
        count = 2 * xs(h)
        for r in range(2):
            row = 2 * h + r

            @pl.when(place != row)
            def _():
                arrived(rhs.at[row], rhs_sem.at[row])

            @pl.when(place == row)
            def _():
                psi_here.wait()

        def step(j, carry):
            there = jnp.logical_not(outer) if h == 0 else jnp.logical_and(outer, j >= 2)

            @pl.when(there)
            def _():
                arrived(ys.at[pl.ds(2 * j, 2)], y_sem.at[j])

            update(2 * h, j)
            update(2 * h + 1, j)
            return carry

        lax.fori_loop(0, count, step, 0)
        for r in range(2):
            if r:
                update(2 * h + 1, count)
            solve(2 * h + r, count + r)
            deliver(h, r, later)

            @pl.when(place == 2 * h + r)
            def _():
                i = count + r
                owned[2 * h + r, 0] = ys[2 * i]
                owned[2 * h + r, 1] = ys[2 * i + 1]

    line(0)
    for s in range(1, 4):
        across(0, s)
    line(1)

    @pl.when(outer)
    def _():
        stage(0, False)

    across(1, 1)
    across(1, 2)

    @pl.when(jnp.logical_not(outer))
    def _():
        stage(0, False)

    across(1, 3)
    stage(1, True)

    writes = []
    for q in range(4):
        @pl.when(place != q)
        def _():
            arrived(owned.at[q], own_sem.at[q])

        for a in range(2):
            write = pltpu.make_async_copy(
                owned.at[q, a], out.at[256 * a : 256 * a + 256, 128 * q : 128 * q + 128],
                local_sem.at[3 + 2 * q + a],
            )
            write.start()
            writes.append(write)
        block = owned[q].reshape(512, 128)
        term = product(block, block, (((1,), (1,)), ((), ())))
        if q == 0:
            part[...] = term
        else:
            part[...] = part[...] + term

    lines = pl.ds(pl.multiple_of(256 * c, 256), 256)
    other = pl.ds(pl.multiple_of(256 - 256 * c, 256), 256)
    send(None, part.at[other], half, half_sem.at[0], half_sem.at[1], device(x, y, z, 1 - c))
    arrived(half, half_sem.at[1])
    half[...] = half[...] + part[lines, :]
    m = 2 * z + y_hi
    for t in range(1, 8):
        to = lax.rem(m + t, 8)
        send(None, half.at[pl.ds(pl.multiple_of(32 * to, 32), 32)], pieces.at[t - 1],
             rs_send.at[t - 1], rs_sem.at[t - 1],
             device(x, 2 * (to % 2) + y_lo, to // 2, c))
    total = half[pl.ds(pl.multiple_of(32 * m, 32), 32), :]
    for t in range(1, 8):
        arrived(pieces.at[t - 1], rs_sem.at[t - 1])
        total = total + pieces[t - 1]
    mine = c * 8 + m
    whole[mine] = total * (1.0 / NG)
    for t in range(1, 8):
        to = lax.rem(m + t, 8)
        send(None, whole.at[mine], whole.at[mine], ag_send.at[t - 1], ag_sem.at[mine],
             device(x, 2 * (to % 2) + y_lo, to // 2, c))
    send(None, whole.at[mine], whole.at[mine], ag_cross.at[0], ag_sem.at[mine],
         device(x, y, z, 1 - c))
    for t in range(1, 8):
        at = c * 8 + lax.rem(m + 8 - t, 8)
        arrived(whole.at[at], ag_sem.at[at])
        send(None, whole.at[at], whole.at[at], ag_cross.at[t], ag_sem.at[at],
             device(x, y, z, 1 - c))
    for t in range(8):
        at = (1 - c) * 8 + t
        arrived(whole.at[at], ag_sem.at[at])
    final = pltpu.make_async_copy(whole, inter, local_sem.at[11])
    final.start()
    for cond, copy in pending:
        if cond is None:
            copy.wait_send()
        else:
            pl.when(cond)(copy.wait_send)
    for row in range(2):
        i = 2 * xs(0) + row
        block = ys.at[pl.ds(2 * i, 2)]
        arrived(block, y_send.at[row])

        @pl.when(place != row)
        def _():
            arrived(block, own_send.at[row])

    for write in writes:
        write.wait()
    final.wait()


def local(psi, lower):
    dma = pltpu.SemaphoreType.DMA
    out, inter = pl.pallas_call(
        kernel,
        out_shape=(
            jax.ShapeDtypeStruct((512, 512), F32),
            jax.ShapeDtypeStruct((16, 32, 512), F32),
        ),
        in_specs=[pl.BlockSpec(memory_space=pl.ANY)] * 2,
        out_specs=(pl.BlockSpec(memory_space=pl.ANY),) * 2,
        scratch_shapes=[
            pltpu.VMEM((128, 256, 256), F32),
            pltpu.VMEM((16, 256, 128), F32),
            pltpu.VMEM((4, 512, 128), F32),
            pltpu.VMEM((4, 2, 256, 128), F32),
            pltpu.VMEM((512, 512), F32),
            pltpu.VMEM((256, 512), F32),
            pltpu.VMEM((7, 32, 512), F32),
            pltpu.VMEM((16, 32, 512), F32),
            pltpu.VMEM((256, 256), F32),
            dma((128,)), dma((12,)), dma((48,)), dma((64,)), dma((2,)), dma((4,)), dma((4,)),
            dma((8,)), dma((4,)), dma((4,)), dma((4,)), dma((2,)), dma((7,)), dma((7,)),
            dma((16,)), dma((7,)), dma((8,)), dma((12,)),
        ],
        compiler_params=pltpu.CompilerParams(
            has_side_effects=True, vmem_limit_bytes=60 * 1024 * 1024
        ),
    )(psi, lower)
    return out, inter.reshape(512, 512)


def solution(mesh):
    return jax.shard_map(
        local,
        mesh=mesh,
        in_specs=(P("band", "ga"), P("band", "ga")),
        out_specs=(P("band", "ga"), P("band", None)),
        check_vma=False,
    )
```

time: 1330 us -> 180 us (0.14)
  waiting for transfers between devices: 1210 us -> 0 us
  Pallas kernels: 0 us -> 174 us
  other arithmetic: 57.2 us -> 0 us
  matrix products: 33 us -> 0 us
    reduce_scatter x9 -> x0, waiting for transfers between devices: 765 us -> none  [the longest x8 692 us: broadcast_by_parts(): own = lax.psum_scatter(padded, axis, scatter_dimension=0, tiled=True)]
    all_gather x10 -> x0, waiting for transfers between devices: 441 us -> none  [the longest x8 312 us: broadcast_by_parts(): lax.all_gather(own, axis, axis=0, tiled=True)[:len(lines)]]
    pallas_call x0 -> x1, Pallas kernels: none -> 174 us  [local(): pl.pallas_call(kernel, out_shape=(jax.ShapeDtypeStruct((512, 512), F32),...]
    another operation x4 -> x0, other arithmetic: 41.5 us -> none  [finish(): return jax.scipy.linalg.solve_triangular(own_tile, rhs, lower=True)]
    dot_general x9 -> x0, matrix products: 29.9 us -> none  [the longest x8 27.1 us: section(): jnp.dot(tile, arrived, precision=lax.Precision.HIGHEST, preferred_element...]
  transfers between devices with their start and end apart: 19 -> 0, of which waited for: 19 -> 0; matrix products, arithmetic and copies ran while one was open for 0% -> 0% of each run, Pallas kernels for 0% -> 0%
where the time goes in v1:
time: 180 us; the launch traced here: 178 us
  Pallas kernels  174 us (97%)
  local copies, waits for them, and re-layouts  3.32 us (2%)
    pallas_call x1, Pallas kernels, local(): pl.pallas_call(kernel, out_shape=(jax.ShapeDtypeStruct((512, 512), F32),...  174 us

profile of v1, /device:TPU:15, one launch (start us, length us, event | category | flops | bytes accessed | tf_op | source)
XLA Modules:
  0.0 178.3 jit_solution(15957802074264383227)
XLA Ops:
  0.6 174.4 %shard_map.41 = (f32[512,512]{1,0:T(8,128)}, f32[16,32,512]{2,1,0:T(8,128)}) custom-call(f32[512,512]{1,0:T(8,128)} %psi.1, f32[512,256]{1,0:T(8,128)} %lower.1), custom_call_target="tpu_custom_call" | custom-call | tf_op jit(solution)/shard_map/pallas_call | solution.py:339
  175.0 0.0 copy-start
  175.0 2.4 %copy.6 = f32[512,512]{1,0:T(8,128)} copy(f32[512,512]{1,0:T(8,128)} %get-tuple-element.8) | data formatting | bytes 2097152
  177.4 0.0 copy-done
  177.4 1.0 copy.7
Async XLA Ops:
  175.0 2.4 %copy-start = (f32[16,32,512]{2,1,0:T(8,128)S(1)}, f32[16,32,512]{2,1,0:T(8,128)}, u32[]{:S(2)}) copy-start(f32[16,32,512]{2,1,0:T(8,128)} %get-tuple-element.5) | copy-start | bytes 3145732

commit v2 on v1

v2 whole, which is shorter than its diff:
```python
import jax
import jax.numpy as jnp
from jax import lax
from jax.experimental import pallas as pl
from jax.experimental.pallas import tpu as pltpu
from jax.sharding import PartitionSpec as P

MESH = pl.DeviceIdType.MESH
F32 = jnp.float32
BF16 = jnp.bfloat16
NG = 8192


def split(a):
    high = a.astype(BF16)
    return high, (a - high.astype(F32)).astype(BF16)


def product(a, b, dims=(((1,), (0,)), ((), ()))):
    ah, al = split(a)
    bh, bl = split(b)

    def dot(p, q):
        return lax.dot_general(p, q, dims, preferred_element_type=F32)

    return dot(ah, bh) + (dot(ah, bl) + dot(al, bh))


def kernel(
    psi, lower, out, inter,
    tiles, ys, rhs, owned, part, half, pieces, whole, inverse,
    tile_sem, ring_sem, cross_sem, pair_sem, swap_sem, rhs_sem, rhs_send,
    y_sem, y_send, own_sem, own_send, half_sem, rs_sem, rs_send, ag_sem, ag_send,
    ag_cross, local_sem,
):
    band = lax.axis_index("band")
    ga = lax.axis_index("ga")
    x, y_lo = band // 2, band % 2
    z, y_hi, c = ga // 4, (ga // 2) % 2, ga % 2
    y = 2 * y_hi + y_lo
    h_own = x // 2
    outer = jnp.logical_or(x == 0, x == 3)
    x_low = jnp.minimum(x, 3 - x)
    place = 2 * h_own + y_lo

    def device(dx, dy, dz, dc):
        return (2 * dx + dy % 2, 4 * dz + 2 * (dy // 2) + dc)

    def xs(h):
        return x_low * (1 - h) + (3 - x_low) * h

    def slot(row, j, a, b):
        return ((row * 8 + j) * 2 + a) * 2 + b

    pending = []

    def send(cond, src, dst, s_sem, r_sem, target, later=True):
        copy = pltpu.make_async_remote_copy(
            src_ref=src, dst_ref=dst, send_sem=s_sem, recv_sem=r_sem,
            device_id=target, device_id_type=MESH,
        )
        if cond is None:
            copy.start()
        else:
            pl.when(cond)(copy.start)
        if later:
            pending.append((cond, copy))
        return copy

    def arrived(ref, sem):
        pltpu.make_async_copy(ref, ref, sem).wait()

    j_own = 2 * z + y_hi
    loads = []
    for a in range(2):
        load = pltpu.make_async_copy(
            lower.at[256 * a : 256 * a + 256, :], tiles.at[slot(place, j_own, a, c)],
            local_sem.at[1 + a],
        )
        load.start()
        loads.append(load)
    psi_here = pltpu.make_async_copy(
        psi.at[:, pl.ds(pl.multiple_of(128 * place, 128), 128)], rhs.at[place], local_sem.at[0]
    )
    psi_here.start()

    def place_of(v):
        return lax.rem(v + 8, 4)

    barrier = pltpu.get_barrier_semaphore()
    friends = [
        (3 - x, y, z, c), (x, 2 * y_hi + 1 - y_lo, z, c), (3 - x, 2 * y_hi + 1 - y_lo, z, c),
        (x + 1 - 2 * (x % 2), y, z, c), (x, y, z, 1 - c),
        (x, place_of(y + 1), z, c), (x, place_of(y - 1), z, c),
        (x, y, place_of(z + 1), c), (x, y, place_of(z - 1), c),
    ] + [
        (x, 2 * (lax.rem(j_own + t, 8) % 2) + y_lo, lax.rem(j_own + t, 8) // 2, c)
        for t in range(1, 8)
    ]
    for friend in friends:
        pl.semaphore_signal(barrier, inc=1, device_id=device(*friend), device_id_type=MESH)
    pl.semaphore_wait(barrier, len(friends))
    for load in loads:
        load.wait()

    def quarter(h, a, k, s):
        sgn = 1 - 2 * a
        yo = place_of(y - sgn * (k * c + s * (1 - c)))
        zo = place_of(z - sgn * (k * (1 - c) + s * c))
        row, j = 2 * h + yo % 2, 2 * zo + yo // 2
        i = 2 * xs(h) + yo % 2
        here = slot(row, j, a, c)
        return here, 2 * j + c <= 2 * i + a

    def await_quarter(h, a, k, s):
        here, real = quarter(h, a, k, s)
        pl.when(real)(lambda: arrived(tiles.at[here], tile_sem.at[here]))

    def along(h, a, k, also=None):
        here, real = quarter(h, a, k, 0)
        sgn = 1 - 2 * a
        cond = real if also is None else jnp.logical_and(real, also)
        ref = tiles.at[here]
        send(cond, ref, ref, ring_sem.at[(h * 2 + a) * 3 + k], tile_sem.at[here],
             device(x, place_of(y + sgn * c), place_of(z + sgn * (1 - c)), c))

    def over(h, a, k, s, also=None):
        here, real = quarter(h, a, k, s)
        sgn = 1 - 2 * a
        cond = real if also is None else jnp.logical_and(real, also)
        ref = tiles.at[here]
        send(cond, ref, ref, cross_sem.at[((h * 2 + a) * 4 + k) * 3 + s], tile_sem.at[here],
             device(x, place_of(y + sgn * (1 - c)), place_of(z + sgn * c), c))

    def to_sibling(h, a, k, s, also=None):
        here, real = quarter(h, a, k, s)
        cond = real if also is None else jnp.logical_and(real, also)
        ref = tiles.at[here]
        send(cond, ref, ref, pair_sem.at[((h * 2 + a) * 4 + k) * 4 + s], tile_sem.at[here],
             device(x, y, z, 1 - c))

    h_other = 1 - h_own
    diagonal = j_own == band

    def own_quarters(ready):
        for a in range(2):
            here, real = quarter(h_own, a, 0, 0)
            send(jnp.logical_and(real, ready(a)), tiles.at[here], tiles.at[here],
                 swap_sem.at[a], tile_sem.at[here], device(3 - x, y, z, c), False)
        for a in range(2):
            along(h_own, a, 0, ready(a))
        for a in range(2):
            over(h_own, a, 0, 0, jnp.logical_and(ready(a), h_own == 0))
            to_sibling(h_own, a, 0, 0, ready(a))

    def send_later():
        for a in range(2):
            here, real = quarter(h_own, a, 0, 0)
            pl.when(real)(lambda: arrived(tiles.at[here], swap_sem.at[a]))

    own_quarters(lambda a: jnp.logical_not(jnp.logical_and(diagonal, c == a)))

    @pl.when(diagonal)
    def _():
        where = slot(place, j_own, c, c)
        rows = lax.broadcasted_iota(jnp.int32, (256, 256), 0)
        cols = lax.broadcasted_iota(jnp.int32, (256, 256), 1)
        tri = tiles[where]
        diag = jnp.where(rows == cols, tri, 0.0)
        down = 1.0 / jnp.sum(diag, axis=1, keepdims=True)
        across = 1.0 / jnp.sum(diag, axis=0, keepdims=True)
        pairs = jnp.logical_and(rows == cols + 1, rows % 2 == 1)
        inverse[...] = jnp.where(rows == cols, down, 0.0) - jnp.where(
            pairs, tri * down * across, 0.0
        )

        def level(k, carry):
            rk, ck = rows >> k, cols >> k
            inside = jnp.logical_and(rk == ck + 1, rk % 2 == 1)
            below = jnp.where(inside, tiles[where], 0.0)
            now = inverse[...]
            inverse[...] = now - product(now, product(below, now))
            return carry

        lax.fori_loop(1, 8, level, 0)
        tiles[where] = inverse[...]

    own_quarters(lambda a: jnp.logical_and(diagonal, c == a))

    for q in range(4):
        send(
            place != q,
            psi.at[:, 128 * q : 128 * q + 128], rhs.at[place],
            rhs_send.at[q], rhs_sem.at[place],
            device(xs(q // 2), 2 * y_hi + q % 2, z, c),
        )

    def line(h, k):
        for a in range(2):
            await_quarter(h, a, k, 0)
            if k < 3:
                along(h, a, k)
            over(h, a, k, 0, h == 0)
            to_sibling(h, a, k, 0)

    def across(h, s):
        for k in range(4):
            for a in range(2):
                await_quarter(h, a, k, s)
                if s < 3:
                    over(h, a, k, s)
                to_sibling(h, a, k, s)

    def tile(row, j, a, b):
        return tiles[slot(row, j, a, b)]

    def from_sibling(row, j, a):
        here = slot(row, j, a, 1 - c)
        arrived(tiles.at[here], tile_sem.at[here])

    def update(row, j):
        for a in range(2):
            from_sibling(row, j, a)
        top, bottom = ys[2 * j], ys[2 * j + 1]
        for a in range(2):
            rhs[row, 256 * a : 256 * a + 256, :] = rhs[row, 256 * a : 256 * a + 256, :] - (
                product(tile(row, j, a, 0), top) + product(tile(row, j, a, 1), bottom)
            )

    def solve(row, i):
        @pl.when(c == 0)
        def _():
            from_sibling(row, i, 1)

        @pl.when(c == 1)
        def _():
            from_sibling(row, i, 0)
            from_sibling(row, i, 1)

        top = product(tile(row, i, 0, 0), rhs[row, 0:256, :])
        ys[2 * i] = top
        bottom = product(
            tile(row, i, 1, 1), rhs[row, 256:512, :] - product(tile(row, i, 1, 0), top)
        )
        ys[2 * i + 1] = bottom

    def deliver(h, r):
        row = 2 * h + r
        i = 2 * xs(h) + r
        block = ys.at[pl.ds(2 * i, 2)]
        send(None if h == 0 else jnp.logical_not(outer), block, block, y_send.at[row],
             y_sem.at[i], device(x + 1 - 2 * (x % 2), y, z, c), False)
        send(place != row, block, owned.at[place], own_send.at[row], own_sem.at[place],
             device(xs(h), 2 * y_hi + r, z, c), False)

        @pl.when(place == row)
        def _():
            owned[row, 0] = ys[2 * i]
            owned[row, 1] = ys[2 * i + 1]

    def await_rhs(h):
        for r in range(2):
            row = 2 * h + r

            @pl.when(place != row)
            def _():
                arrived(rhs.at[row], rhs_sem.at[row])

            @pl.when(place == row)
            def _():
                psi_here.wait()

    def await_y(j):
        arrived(ys.at[pl.ds(2 * j, 2)], y_sem.at[j])

    def by_columns(h, arriving):
        count = 2 * xs(h)

        def step(j, carry):
            pl.when(arriving(j))(lambda: await_y(j))
            update(2 * h, j)
            update(2 * h + 1, j)
            return carry

        lax.fori_loop(0, count, step, 0)
        solve(2 * h, count)
        deliver(h, 0)
        update(2 * h + 1, count)
        solve(2 * h + 1, count + 1)
        deliver(h, 1)

    def by_rows(h):
        count = 2 * xs(h)
        for r in range(2):
            def step(j, carry, r=r):
                update(2 * h + r, j)
                return carry

            lax.fori_loop(0, count + r, step, 0)
            solve(2 * h + r, count + r)
            deliver(h, r)

    with jax.named_scope("line"):
        line(h_own, 1)
        line(h_other, 0)
        line(h_own, 2)
        line(h_other, 1)
        line(h_own, 3)
        line(h_other, 2)
        line(h_other, 3)
    with jax.named_scope("across01"):
        across(0, 1)
        for k in range(4):
            for a in range(2):
                over(1, a, k, 0)
    with jax.named_scope("across02"):
        across(0, 2)
    with jax.named_scope("across03"):
        across(0, 3)
        await_rhs(0)

    with jax.named_scope("early"):
        @pl.when(outer)
        def _():
            by_columns(0, lambda j: j < 0)

    with jax.named_scope("across11"):
        across(1, 1)
    with jax.named_scope("across12"):
        across(1, 2)
        await_rhs(1)

    with jax.named_scope("inner"):
        @pl.when(jnp.logical_not(outer))
        def _():
            by_columns(0, lambda j: j >= 0)

    with jax.named_scope("across13"):
        across(1, 3)
    with jax.named_scope("last"):
        @pl.when(outer)
        def _():
            by_columns(1, lambda j: j >= 2)

        @pl.when(jnp.logical_not(outer))
        def _():
            by_rows(1)

    writes = []
    with jax.named_scope("product"):
        for q in range(4):
            pl.when(place != q)(lambda: arrived(owned.at[q], own_sem.at[q]))
            for a in range(2):
                write = pltpu.make_async_copy(
                    owned.at[q, a], out.at[256 * a : 256 * a + 256, 128 * q : 128 * q + 128],
                    local_sem.at[3 + 2 * q + a],
                )
                write.start()
                writes.append(write)
            block = owned[q].reshape(512, 128)
            term = product(block, block, (((1,), (1,)), ((), ())))
            if q == 0:
                part[...] = term
            else:
                part[...] = part[...] + term

    lines = pl.ds(pl.multiple_of(256 * c, 256), 256)
    other = pl.ds(pl.multiple_of(256 - 256 * c, 256), 256)
    with jax.named_scope("halves"):
        send(None, part.at[other], half, half_sem.at[0], half_sem.at[1], device(x, y, z, 1 - c))
        arrived(half, half_sem.at[1])
        half[...] = half[...] + part[lines, :]
    m = j_own
    with jax.named_scope("scatter"):
        for t in range(1, 8):
            to = lax.rem(m + t, 8)
            send(None, half.at[pl.ds(pl.multiple_of(32 * to, 32), 32)], pieces.at[t - 1],
                 rs_send.at[t - 1], rs_sem.at[t - 1],
                 device(x, 2 * (to % 2) + y_lo, to // 2, c))
        total = half[pl.ds(pl.multiple_of(32 * m, 32), 32), :]
        for t in range(1, 8):
            arrived(pieces.at[t - 1], rs_sem.at[t - 1])
            total = total + pieces[t - 1]
        mine = c * 8 + m
        whole[mine] = total * (1.0 / NG)
    with jax.named_scope("spread"):
        for t in range(1, 8):
            to = lax.rem(m + t, 8)
            send(None, whole.at[mine], whole.at[mine], ag_send.at[t - 1], ag_sem.at[mine],
                 device(x, 2 * (to % 2) + y_lo, to // 2, c))
        send(None, whole.at[mine], whole.at[mine], ag_cross.at[0], ag_sem.at[mine],
             device(x, y, z, 1 - c))
        for t in range(1, 8):
            at = c * 8 + lax.rem(m + 8 - t, 8)
            arrived(whole.at[at], ag_sem.at[at])
            send(None, whole.at[at], whole.at[at], ag_cross.at[t], ag_sem.at[at],
                 device(x, y, z, 1 - c))
        for t in range(8):
            at = (1 - c) * 8 + t
            arrived(whole.at[at], ag_sem.at[at])
    final = pltpu.make_async_copy(whole, inter, local_sem.at[11])
    final.start()
    for cond, copy in pending:
        if cond is None:
            copy.wait_send()
        else:
            pl.when(cond)(copy.wait_send)
    send_later()
    for row in range(4):
        i = 2 * xs(row // 2) + row % 2
        block = ys.at[pl.ds(2 * i, 2)]
        if row < 2:
            arrived(block, y_send.at[row])
        else:
            pl.when(jnp.logical_not(outer))(lambda: arrived(block, y_send.at[row]))
        pl.when(place != row)(lambda: arrived(block, own_send.at[row]))
    for write in writes:
        write.wait()
    final.wait()


def local(psi, lower):
    dma = pltpu.SemaphoreType.DMA
    out, inter = pl.pallas_call(
        kernel,
        out_shape=(
            jax.ShapeDtypeStruct((512, 512), F32),
            jax.ShapeDtypeStruct((16, 32, 512), F32),
        ),
        in_specs=[pl.BlockSpec(memory_space=pl.ANY)] * 2,
        out_specs=(pl.BlockSpec(memory_space=pl.ANY),) * 2,
        scratch_shapes=[
            pltpu.VMEM((128, 256, 256), F32),
            pltpu.VMEM((16, 256, 128), F32),
            pltpu.VMEM((4, 512, 128), F32),
            pltpu.VMEM((4, 2, 256, 128), F32),
            pltpu.VMEM((512, 512), F32),
            pltpu.VMEM((256, 512), F32),
            pltpu.VMEM((7, 32, 512), F32),
            pltpu.VMEM((16, 32, 512), F32),
            pltpu.VMEM((256, 256), F32),
            dma((128,)), dma((12,)), dma((48,)), dma((64,)), dma((2,)), dma((4,)), dma((4,)),
            dma((8,)), dma((4,)), dma((4,)), dma((4,)), dma((2,)), dma((7,)), dma((7,)),
            dma((16,)), dma((7,)), dma((8,)), dma((12,)),
        ],
        compiler_params=pltpu.CompilerParams(
            has_side_effects=True, collective_id=0, vmem_limit_bytes=60 * 1024 * 1024
        ),
    )(psi, lower)
    return out, inter.reshape(512, 512)


def solution(mesh):
    return jax.shard_map(
        local,
        mesh=mesh,
        in_specs=(P("band", "ga"), P("band", "ga")),
        out_specs=(P("band", "ga"), P("band", None)),
        check_vma=False,
    )
```

time: 180 us -> 151 us (0.84)
  Pallas kernels: 174 us -> 147 us
    pallas_call x1, Pallas kernels: 174 us -> 147 us  [local(): pl.pallas_call(kernel, out_shape=(jax.ShapeDtypeStruct((512, 512), F32),...]
where the time goes in v2:
time: 151 us
  Pallas kernels  147 us (97%)
  local copies, waits for them, and re-layouts  3.32 us (2%)
    pallas_call x1, Pallas kernels, local(): pl.pallas_call(kernel, out_shape=(jax.ShapeDtypeStruct((512, 512), F32),...  147 us
    unnamed x4, local copies, waits for them, and re-layouts  3.32 us

profile of v2, /device:TPU:15, one launch (start us, length us, event | category | flops | bytes accessed | tf_op | source)
XLA Modules:
  0.0 151.1 jit_solution(10535846017141067793)
XLA Ops:
  0.6 147.1 %shard_map.41 = (f32[512,512]{1,0:T(8,128)}, f32[16,32,512]{2,1,0:T(8,128)}) custom-call(f32[512,512]{1,0:T(8,128)} %psi.1, f32[512,256]{1,0:T(8,128)} %lower.1), custom_call_target="tpu_custom_call" | custom-call | tf_op jit(solution)/shard_map/pallas_call | solution.py:424
  147.8 0.0 copy-start
  147.8 2.4 %copy.6 = f32[512,512]{1,0:T(8,128)} copy(f32[512,512]{1,0:T(8,128)} %get-tuple-element.8) | data formatting | bytes 2097152
  150.1 0.0 copy-done
  150.1 1.0 copy.7
Async XLA Ops:
  147.8 2.4 %copy-start = (f32[16,32,512]{2,1,0:T(8,128)S(1)}, f32[16,32,512]{2,1,0:T(8,128)}, u32[]{:S(2)}) copy-start(f32[16,32,512]{2,1,0:T(8,128)} %get-tuple-element.5) | copy-start | bytes 3145732

commit v3 on v2

--- a/solution.py
+++ b/solution.py
@@ -153,6 +153,14 @@
             over(h_own, a, 0, 0, jnp.logical_and(ready(a), h_own == 0))
             to_sibling(h_own, a, 0, 0, ready(a))
 
+    def finish_sends():
+        for cond, copy in pending:
+            if cond is None:
+                copy.wait_send()
+            else:
+                pl.when(cond)(copy.wait_send)
+        pending.clear()
+
     def send_later():
         for a in range(2):
             here, real = quarter(h_own, a, 0, 0)
@@ -187,13 +195,14 @@
 
     own_quarters(lambda a: jnp.logical_and(diagonal, c == a))
 
-    for q in range(4):
-        send(
-            place != q,
-            psi.at[:, 128 * q : 128 * q + 128], rhs.at[place],
-            rhs_send.at[q], rhs_sem.at[place],
-            device(xs(q // 2), 2 * y_hi + q % 2, z, c),
-        )
+    def share_rhs(when):
+        for q in range(4):
+            send(
+                jnp.logical_and(place != q, when),
+                psi.at[:, 128 * q : 128 * q + 128], rhs.at[place],
+                rhs_send.at[q], rhs_sem.at[place],
+                device(xs(q // 2), 2 * y_hi + q % 2, z, c),
+            )
 
     def line(h, k):
         for a in range(2):
@@ -227,7 +236,24 @@
                 product(tile(row, j, a, 0), top) + product(tile(row, j, a, 1), bottom)
             )
 
-    def solve(row, i):
+    def deliver(h, r, part_no):
+        row = 2 * h + r
+        i = 2 * xs(h) + r
+        block = ys.at[2 * i + part_no]
+        send(None if h == 0 else jnp.logical_not(outer), block, block,
+             y_send.at[2 * row + part_no], y_sem.at[2 * i + part_no],
+             device(x + 1 - 2 * (x % 2), y, z, c), False)
+        send(place != row, block, owned.at[place, part_no], own_send.at[2 * row + part_no],
+             own_sem.at[place, part_no], device(xs(h), 2 * y_hi + r, z, c), False)
+
+        @pl.when(place == row)
+        def _():
+            owned[row, part_no] = ys[2 * i + part_no]
+
+    def solve(h, r):
+        row = 2 * h + r
+        i = 2 * xs(h) + r
+
         @pl.when(c == 0)
         def _():
             from_sibling(row, i, 1)
@@ -239,24 +265,12 @@
 
         top = product(tile(row, i, 0, 0), rhs[row, 0:256, :])
         ys[2 * i] = top
+        deliver(h, r, 0)
         bottom = product(
             tile(row, i, 1, 1), rhs[row, 256:512, :] - product(tile(row, i, 1, 0), top)
         )
         ys[2 * i + 1] = bottom
-
-    def deliver(h, r):
-        row = 2 * h + r
-        i = 2 * xs(h) + r
-        block = ys.at[pl.ds(2 * i, 2)]
-        send(None if h == 0 else jnp.logical_not(outer), block, block, y_send.at[row],
-             y_sem.at[i], device(x + 1 - 2 * (x % 2), y, z, c), False)
-        send(place != row, block, owned.at[place], own_send.at[row], own_sem.at[place],
-             device(xs(h), 2 * y_hi + r, z, c), False)
-
-        @pl.when(place == row)
-        def _():
-            owned[row, 0] = ys[2 * i]
-            owned[row, 1] = ys[2 * i + 1]
+        deliver(h, r, 1)
 
     def await_rhs(h):
         for r in range(2):
@@ -271,7 +285,8 @@
                 psi_here.wait()
 
     def await_y(j):
-        arrived(ys.at[pl.ds(2 * j, 2)], y_sem.at[j])
+        for part_no in range(2):
+            arrived(ys.at[2 * j + part_no], y_sem.at[2 * j + part_no])
 
     def by_columns(h, arriving):
         count = 2 * xs(h)
@@ -283,11 +298,9 @@
             return carry
 
         lax.fori_loop(0, count, step, 0)
-        solve(2 * h, count)
-        deliver(h, 0)
+        solve(h, 0)
         update(2 * h + 1, count)
-        solve(2 * h + 1, count + 1)
-        deliver(h, 1)
+        solve(h, 1)
 
     def by_rows(h):
         count = 2 * xs(h)
@@ -297,24 +310,28 @@
                 return carry
 
             lax.fori_loop(0, count + r, step, 0)
-            solve(2 * h + r, count + r)
-            deliver(h, r)
-
+            solve(h, r)
+
+    def begin_over(h):
+        for k in range(4):
+            for a in range(2):
+                over(h, a, k, 0)
+
+    share_rhs(h_own == 0)
     with jax.named_scope("line"):
-        line(h_own, 1)
         line(h_other, 0)
-        line(h_own, 2)
-        line(h_other, 1)
-        line(h_own, 3)
-        line(h_other, 2)
-        line(h_other, 3)
+        line(0, 1)
+        line(1, 1)
+        line(0, 2)
+        line(0, 3)
     with jax.named_scope("across01"):
         across(0, 1)
-        for k in range(4):
-            for a in range(2):
-                over(1, a, k, 0)
+        line(1, 2)
     with jax.named_scope("across02"):
         across(0, 2)
+        line(1, 3)
+        begin_over(1)
+        share_rhs(h_own == 1)
     with jax.named_scope("across03"):
         across(0, 3)
         await_rhs(0)
@@ -346,77 +363,96 @@
         def _():
             by_rows(1)
 
+    with jax.named_scope("settle"):
+        finish_sends()
+        send_later()
+        for row in range(4):
+            for part_no in range(2):
+                block = ys.at[2 * (2 * xs(row // 2) + row % 2) + part_no]
+                sem = y_send.at[2 * row + part_no]
+                if row < 2:
+                    arrived(block, sem)
+                else:
+                    pl.when(jnp.logical_not(outer))(lambda: arrived(block, sem))
+                pl.when(place != row)(lambda: arrived(block, own_send.at[2 * row + part_no]))
+
     writes = []
     with jax.named_scope("product"):
-        for q in range(4):
-            pl.when(place != q)(lambda: arrived(owned.at[q], own_sem.at[q]))
+        beside = place + 1 - 2 * (place % 2)
+        for n, q in enumerate(
+            (place, beside, lax.rem(place + 2, 4), lax.rem(beside + 2, 4))
+        ):
             for a in range(2):
+                if n:
+                    arrived(owned.at[q, a], own_sem.at[q, a])
                 write = pltpu.make_async_copy(
-                    owned.at[q, a], out.at[256 * a : 256 * a + 256, 128 * q : 128 * q + 128],
-                    local_sem.at[3 + 2 * q + a],
+                    owned.at[q, a],
+                    out.at[
+                        256 * a : 256 * a + 256, pl.ds(pl.multiple_of(128 * q, 128), 128)
+                    ],
+                    local_sem.at[3 + 2 * n + a],
                 )
                 write.start()
                 writes.append(write)
             block = owned[q].reshape(512, 128)
-            term = product(block, block, (((1,), (1,)), ((), ())))
-            if q == 0:
-                part[...] = term
-            else:
-                part[...] = part[...] + term
-
-    lines = pl.ds(pl.multiple_of(256 * c, 256), 256)
-    other = pl.ds(pl.multiple_of(256 - 256 * c, 256), 256)
+            at = 0
+            for r in range(4):
+                term = product(
+                    block[128 * r : 128 * r + 128], block[: 128 * r + 128],
+                    (((1,), (1,)), ((), ())),
+                )
+                for s in range(r + 1):
+                    here = term[:, 128 * s : 128 * s + 128]
+                    part[at] = here if n == 0 else part[at] + here
+                    at += 1
+
     with jax.named_scope("halves"):
-        send(None, part.at[other], half, half_sem.at[0], half_sem.at[1], device(x, y, z, 1 - c))
+        send(None, part.at[pl.ds(5 - 5 * c, 5)], half, half_sem.at[0], half_sem.at[1],
+             device(x, y, z, 1 - c))
         arrived(half, half_sem.at[1])
-        half[...] = half[...] + part[lines, :]
+        half[...] = half[...] + part[pl.ds(5 * c, 5)]
     m = j_own
+
+    def lines(of):
+        return pl.ds(pl.multiple_of(16 * of, 16), 16)
+
     with jax.named_scope("scatter"):
         for t in range(1, 8):
             to = lax.rem(m + t, 8)
-            send(None, half.at[pl.ds(pl.multiple_of(32 * to, 32), 32)], pieces.at[t - 1],
+            send(None, half.at[:, lines(to)], pieces.at[t - 1],
                  rs_send.at[t - 1], rs_sem.at[t - 1],
                  device(x, 2 * (to % 2) + y_lo, to // 2, c))
-        total = half[pl.ds(pl.multiple_of(32 * m, 32), 32), :]
+        total = half[:, lines(m), :]
         for t in range(1, 8):
             arrived(pieces.at[t - 1], rs_sem.at[t - 1])
             total = total + pieces[t - 1]
-        mine = c * 8 + m
-        whole[mine] = total * (1.0 / NG)
+        whole[c, :, lines(m), :] = total * (1.0 / NG)
     with jax.named_scope("spread"):
+        def share(core, of, s_sem, target):
+            ref = whole.at[core, :, lines(of)]
+            send(None, ref, ref, s_sem, ag_sem.at[core * 8 + of], target)
+
         for t in range(1, 8):
             to = lax.rem(m + t, 8)
-            send(None, whole.at[mine], whole.at[mine], ag_send.at[t - 1], ag_sem.at[mine],
-                 device(x, 2 * (to % 2) + y_lo, to // 2, c))
-        send(None, whole.at[mine], whole.at[mine], ag_cross.at[0], ag_sem.at[mine],
-             device(x, y, z, 1 - c))
+            share(c, m, ag_send.at[t - 1], device(x, 2 * (to % 2) + y_lo, to // 2, c))
+        share(c, m, ag_cross.at[0], device(x, y, z, 1 - c))
         for t in range(1, 8):
-            at = c * 8 + lax.rem(m + 8 - t, 8)
-            arrived(whole.at[at], ag_sem.at[at])
-            send(None, whole.at[at], whole.at[at], ag_cross.at[t], ag_sem.at[at],
-                 device(x, y, z, 1 - c))
-        for t in range(8):
-            at = (1 - c) * 8 + t
-            arrived(whole.at[at], ag_sem.at[at])
-    final = pltpu.make_async_copy(whole, inter, local_sem.at[11])
-    final.start()
-    for cond, copy in pending:
-        if cond is None:
-            copy.wait_send()
-        else:
-            pl.when(cond)(copy.wait_send)
-    send_later()
-    for row in range(4):
-        i = 2 * xs(row // 2) + row % 2
-        block = ys.at[pl.ds(2 * i, 2)]
-        if row < 2:
-            arrived(block, y_send.at[row])
-        else:
-            pl.when(jnp.logical_not(outer))(lambda: arrived(block, y_send.at[row]))
-        pl.when(place != row)(lambda: arrived(block, own_send.at[row]))
+            of = lax.rem(m + 8 - t, 8)
+            arrived(whole.at[c, :, lines(of)], ag_sem.at[c * 8 + of])
+            share(c, of, ag_cross.at[t], device(x, y, z, 1 - c))
+        for of in range(8):
+            arrived(whole.at[1 - c, :, lines(of)], ag_sem.at[(1 - c) * 8 + of])
+        at = 0
+        for r in range(4):
+            for s in range(r + 1):
+                block = whole[at // 5, at % 5]
+                inter[128 * r : 128 * r + 128, 128 * s : 128 * s + 128] = block
+                if s < r:
+                    inter[128 * s : 128 * s + 128, 128 * r : 128 * r + 128] = block.T
+                at += 1
+    finish_sends()
     for write in writes:
         write.wait()
-    final.wait()
 
 
 def local(psi, lower):
@@ -424,30 +460,30 @@
     out, inter = pl.pallas_call(
         kernel,
         out_shape=(
-            jax.ShapeDtypeStruct((512, 512), F32),
-            jax.ShapeDtypeStruct((16, 32, 512), F32),
+            pltpu.VMEM((512, 512), F32),
+            pltpu.VMEM((512, 512), F32),
         ),
         in_specs=[pl.BlockSpec(memory_space=pl.ANY)] * 2,
-        out_specs=(pl.BlockSpec(memory_space=pl.ANY),) * 2,
+        out_specs=(pl.BlockSpec(memory_space=pltpu.VMEM),) * 2,
         scratch_shapes=[
             pltpu.VMEM((128, 256, 256), F32),
             pltpu.VMEM((16, 256, 128), F32),
             pltpu.VMEM((4, 512, 128), F32),
             pltpu.VMEM((4, 2, 256, 128), F32),
-            pltpu.VMEM((512, 512), F32),
-            pltpu.VMEM((256, 512), F32),
-            pltpu.VMEM((7, 32, 512), F32),
-            pltpu.VMEM((16, 32, 512), F32),
+            pltpu.VMEM((10, 128, 128), F32),
+            pltpu.VMEM((5, 128, 128), F32),
+            pltpu.VMEM((7, 5, 16, 128), F32),
+            pltpu.VMEM((2, 5, 128, 128), F32),
             pltpu.VMEM((256, 256), F32),
             dma((128,)), dma((12,)), dma((48,)), dma((64,)), dma((2,)), dma((4,)), dma((4,)),
-            dma((8,)), dma((4,)), dma((4,)), dma((4,)), dma((2,)), dma((7,)), dma((7,)),
+            dma((16,)), dma((8,)), dma((4, 2)), dma((8,)), dma((2,)), dma((7,)), dma((7,)),
             dma((16,)), dma((7,)), dma((8,)), dma((12,)),
         ],
         compiler_params=pltpu.CompilerParams(
             has_side_effects=True, collective_id=0, vmem_limit_bytes=60 * 1024 * 1024
         ),
     )(psi, lower)
-    return out, inter.reshape(512, 512)
+    return out, inter
 
 
 def solution(mesh):

time: 151 us -> 146 us (0.967); the launches traced: 151 us -> 145 us
  Pallas kernels: 147 us -> 142 us
    pallas_call x1, Pallas kernels: 147 us -> 142 us  [local(): pl.pallas_call(kernel, out_shape=(pltpu.VMEM((512, 512), F32), pltpu.VMEM...]
    unnamed x4 -> x2, local copies, waits for them, and re-layouts: 3.32 us -> 1.94 us
where the time goes in v3:
time: 146 us; the launch traced here: 145 us
  Pallas kernels  142 us (97%)
  local copies, waits for them, and re-layouts  1.94 us (1%)
    pallas_call x1, Pallas kernels, local(): pl.pallas_call(kernel, out_shape=(pltpu.VMEM((512, 512), F32), pltpu.VMEM...  142 us

profile of v3, /device:TPU:15, one launch (start us, length us, event | category | flops | bytes accessed | tf_op | source)
XLA Modules:
  0.0 144.5 jit_solution(13168238620298541908)
XLA Ops:
  0.6 141.9 %shard_map.41 = (f32[512,512]{1,0:T(8,128)S(1)}, f32[512,512]{1,0:T(8,128)S(1)}) custom-call(f32[512,512]{1,0:T(8,128)} %psi.1, f32[512,256]{1,0:T(8,128)} %lower.1), custom_call_target="tpu_custom_call" | custom-call | tf_op jit(solution)/shard_map/pallas_call | solution.py:460
  142.6 1.0 copy.6
  143.5 1.0 copy.7

commit v4 on v3

--- a/solution.py
+++ b/solution.py
@@ -10,6 +10,28 @@
 BF16 = jnp.bfloat16
 NG = 8192
 
+EVENTS = (
+    (405115079, 138699458, 461177167, 540649354, 326504717, 695371218, 357657612,
+     602061930, 867409058, 882306733, 1037815163, 1054767524, 4079),
+    (421552280, 154706183, 51775376, 525972442, 295774283, 695256916, 390912688,
+     952720171, 986896625, 668702899, 905070958, 1037987771, 4079),
+    (537428547, 86553697, 676088400, 339051673, 113447715, 128820586, 266742939,
+     476001720, 764594510, 899395293, 800714023, 937152351, 4094),
+    (170143880, 276869381, 122324065, 322081165, 408049898, 246216880, 616932697,
+     850754028, 870431126, 884709167, 519023965, 1054830367, 4093),
+    (9079395, 723717185, 949397769, 300360755, 655282818, 422414764, 988619076,
+     213599477, 102553263, 937150164, 477422973, 402646415, 2014),
+    (697182720, 613714561, 180556139, 43696324, 868932041, 959639056, 114340335,
+     1005134965, 926377492, 256886350, 486106813, 492692827, 4063),
+    (419860520, 52791459, 264574160, 734032607, 605664712, 313058149, 98936670,
+     751313592, 72963852, 871029140, 936856507, 1073471271, 3062),
+    (580917824, 588808450, 705459150, 177333925, 414043185, 455393631, 429554443,
+     347432080, 944193117, 844946351, 1005280531, 1039228406, 4094),
+)
+SHARE_AT = (19, 23, 22, 23, 22, 23, 22, 26)
+STAGE_AT = (35, 42, 59, 59, 62, 62, 49, 59)
+EVENT_COUNT = (62, 62, 62, 62, 62, 62, 62, 62)
+
 
 def split(a):
     high = a.astype(BF16)
@@ -26,10 +48,18 @@
     return dot(ah, bh) + (dot(ah, bl) + dot(al, bh))
 
 
+def narrow_product(a, b):
+    ah, al = split(a)
+    bh, bl = split(b)
+    wide = jnp.dot(ah, jnp.concatenate([bh, bl], axis=1), preferred_element_type=F32)
+    rest = jnp.dot(al, bh, preferred_element_type=F32)
+    return wide[:, :128] + (wide[:, 128:] + rest)
+
+
 def kernel(
     psi, lower, out, inter,
     tiles, ys, rhs, owned, part, half, pieces, whole, inverse,
-    tile_sem, ring_sem, cross_sem, pair_sem, swap_sem, rhs_sem, rhs_send,
+    tile_sem, ring_sem, back_sem, cross_sem, return_sem, pair_sem, swap_sem, rhs_sem, rhs_send,
     y_sem, y_send, own_sem, own_send, half_sem, rs_sem, rs_send, ag_sem, ag_send,
     ag_cross, local_sem,
 ):
@@ -112,46 +142,55 @@
         here = slot(row, j, a, c)
         return here, 2 * j + c <= 2 * i + a
 
-    def await_quarter(h, a, k, s):
-        here, real = quarter(h, a, k, s)
-        pl.when(real)(lambda: arrived(tiles.at[here], tile_sem.at[here]))
-
-    def along(h, a, k, also=None):
-        here, real = quarter(h, a, k, 0)
-        sgn = 1 - 2 * a
-        cond = real if also is None else jnp.logical_and(real, also)
-        ref = tiles.at[here]
-        send(cond, ref, ref, ring_sem.at[(h * 2 + a) * 3 + k], tile_sem.at[here],
-             device(x, place_of(y + sgn * c), place_of(z + sgn * (1 - c)), c))
-
-    def over(h, a, k, s, also=None):
+    diagonal = j_own == band
+
+    def both(*conds):
+        out = conds[0]
+        for cond in conds[1:]:
+            out = jnp.logical_and(out, cond)
+        return out
+
+    def by_pair(h, k, s):
+        far = jnp.logical_or(k > 0, s > 0)
+        return jnp.logical_or(
+            both(outer, h == 0, far),
+            both(k == 0, s > 0, jnp.logical_or(h == 1, jnp.logical_not(outer))),
+        )
+
+    def copies(h, a, k, s):
         here, real = quarter(h, a, k, s)
         sgn = 1 - 2 * a
-        cond = real if also is None else jnp.logical_and(real, also)
+        ours = h == h_own
+        short1 = short2 = both(outer, h == 0)
         ref = tiles.at[here]
-        send(cond, ref, ref, cross_sem.at[((h * 2 + a) * 4 + k) * 3 + s], tile_sem.at[here],
-             device(x, place_of(y + sgn * (1 - c)), place_of(z + sgn * c), c))
-
-    def to_sibling(h, a, k, s, also=None):
-        here, real = quarter(h, a, k, s)
-        cond = real if also is None else jnp.logical_and(real, also)
-        ref = tiles.at[here]
-        send(cond, ref, ref, pair_sem.at[((h * 2 + a) * 4 + k) * 4 + s], tile_sem.at[here],
-             device(x, y, z, 1 - c))
-
-    h_other = 1 - h_own
-    diagonal = j_own == band
-
-    def own_quarters(ready):
-        for a in range(2):
-            here, real = quarter(h_own, a, 0, 0)
-            send(jnp.logical_and(real, ready(a)), tiles.at[here], tiles.at[here],
-                 swap_sem.at[a], tile_sem.at[here], device(3 - x, y, z, c), False)
-        for a in range(2):
-            along(h_own, a, 0, ready(a))
-        for a in range(2):
-            over(h_own, a, 0, 0, jnp.logical_and(ready(a), h_own == 0))
-            to_sibling(h_own, a, 0, 0, ready(a))
+
+        def along(m):
+            return device(x, place_of(y + m * c), place_of(z + m * (1 - c)), c)
+
+        def over(m):
+            return device(x, place_of(y + m * (1 - c)), place_of(z + m * c), c)
+
+        def ring(k2, s2):
+            return both(real, jnp.logical_or(ours, jnp.logical_not(by_pair(h, k2, s2))))
+
+        last1 = 3 - short1.astype(jnp.int32)
+        last2 = 3 - short2.astype(jnp.int32)
+        near = both(k == 0, s == 0)
+        line = (h * 4 + k) * 2 + a
+        for cond, sem, target in (
+            (both(real, ours, jnp.logical_or(near, by_pair(h, k, s))),
+             swap_sem.at[line * 4 + s], device(3 - x, y, z, c)),
+            (both(ring(k + 1, 0), s == 0, k < last1),
+             ring_sem.at[line], along(sgn)),
+            (both(ring(3, 0), near, short1), back_sem.at[h * 2 + a], along(-sgn)),
+            (both(ring(k, s + 1), s < last2), cross_sem.at[line * 4 + s], over(sgn)),
+            (both(ring(k, 3), s == 0, short2), return_sem.at[line], over(-sgn)),
+            (real, pair_sem.at[line * 4 + s], device(x, y, z, 1 - c)),
+        ):
+            yield cond, pltpu.make_async_remote_copy(
+                src_ref=ref, dst_ref=ref, send_sem=sem, recv_sem=tile_sem.at[here],
+                device_id=target, device_id_type=MESH,
+            )
 
     def finish_sends():
         for cond, copy in pending:
@@ -161,12 +200,44 @@
                 pl.when(cond)(copy.wait_send)
         pending.clear()
 
-    def send_later():
+    def own_quarters(ready):
         for a in range(2):
-            here, real = quarter(h_own, a, 0, 0)
-            pl.when(real)(lambda: arrived(tiles.at[here], swap_sem.at[a]))
-
-    own_quarters(lambda a: jnp.logical_not(jnp.logical_and(diagonal, c == a)))
+            for cond, copy in copies(h_own, a, 0, 0):
+                pl.when(both(cond, ready(a)))(copy.start)
+
+    def decode(code):
+        return code // 32, code % 2, (code // 8) % 4, (code // 2) % 4
+
+    kind = 2 * x + c
+
+    def by_kind(values):
+        out = jnp.int32(values[0])
+        for n, value in enumerate(values[1:]):
+            out = jnp.where(kind == n + 1, jnp.int32(value), out)
+        return out
+
+    words = [by_kind(word) for word in zip(*EVENTS)]
+
+    def event(n, carry):
+        which = n // 5
+        word = words[0]
+        for at, other in enumerate(words[1:]):
+            word = jnp.where(which == at + 1, other, word)
+        h, a, k, s = decode(lax.shift_right_logical(word, 6 * (n % 5)) % 64)
+        here, real = quarter(h, a, k, s)
+        pl.when(both(real, jnp.logical_not(both(h == h_own, k == 0, s == 0))))(
+            lambda: arrived(tiles.at[here], tile_sem.at[here])
+        )
+        for cond, copy in copies(h, a, k, s):
+            pl.when(cond)(copy.start)
+        return carry
+
+    def sent(code, carry):
+        for cond, copy in copies(*decode(code)):
+            pl.when(cond)(copy.wait_send)
+        return carry
+
+    own_quarters(lambda a: jnp.logical_not(both(diagonal, c == a)))
 
     @pl.when(diagonal)
     def _():
@@ -193,7 +264,7 @@
         lax.fori_loop(1, 8, level, 0)
         tiles[where] = inverse[...]
 
-    own_quarters(lambda a: jnp.logical_and(diagonal, c == a))
+    own_quarters(lambda a: both(diagonal, c == a))
 
     def share_rhs(when):
         for q in range(4):
@@ -204,22 +275,6 @@
                 device(xs(q // 2), 2 * y_hi + q % 2, z, c),
             )
 
-    def line(h, k):
-        for a in range(2):
-            await_quarter(h, a, k, 0)
-            if k < 3:
-                along(h, a, k)
-            over(h, a, k, 0, h == 0)
-            to_sibling(h, a, k, 0)
-
-    def across(h, s):
-        for k in range(4):
-            for a in range(2):
-                await_quarter(h, a, k, s)
-                if s < 3:
-                    over(h, a, k, s)
-                to_sibling(h, a, k, s)
-
     def tile(row, j, a, b):
         return tiles[slot(row, j, a, b)]
 
@@ -233,7 +288,7 @@
         top, bottom = ys[2 * j], ys[2 * j + 1]
         for a in range(2):
             rhs[row, 256 * a : 256 * a + 256, :] = rhs[row, 256 * a : 256 * a + 256, :] - (
-                product(tile(row, j, a, 0), top) + product(tile(row, j, a, 1), bottom)
+                narrow_product(tile(row, j, a, 0), top) + narrow_product(tile(row, j, a, 1), bottom)
             )
 
     def deliver(h, r, part_no):
@@ -263,11 +318,11 @@
             from_sibling(row, i, 0)
             from_sibling(row, i, 1)
 
-        top = product(tile(row, i, 0, 0), rhs[row, 0:256, :])
+        top = narrow_product(tile(row, i, 0, 0), rhs[row, 0:256, :])
         ys[2 * i] = top
         deliver(h, r, 0)
-        bottom = product(
-            tile(row, i, 1, 1), rhs[row, 256:512, :] - product(tile(row, i, 1, 0), top)
+        bottom = narrow_product(
+            tile(row, i, 1, 1), rhs[row, 256:512, :] - narrow_product(tile(row, i, 1, 0), top)
         )
         ys[2 * i + 1] = bottom
         deliver(h, r, 1)
@@ -312,49 +367,21 @@
             lax.fori_loop(0, count + r, step, 0)
             solve(h, r)
 
-    def begin_over(h):
-        for k in range(4):
-            for a in range(2):
-                over(h, a, k, 0)
-
+    share_at, stage_at, count = by_kind(SHARE_AT), by_kind(STAGE_AT), by_kind(EVENT_COUNT)
     share_rhs(h_own == 0)
-    with jax.named_scope("line"):
-        line(h_other, 0)
-        line(0, 1)
-        line(1, 1)
-        line(0, 2)
-        line(0, 3)
-    with jax.named_scope("across01"):
-        across(0, 1)
-        line(1, 2)
-    with jax.named_scope("across02"):
-        across(0, 2)
-        line(1, 3)
-        begin_over(1)
-        share_rhs(h_own == 1)
-    with jax.named_scope("across03"):
-        across(0, 3)
+    with jax.named_scope("first"):
+        lax.fori_loop(0, share_at, event, 0)
+    share_rhs(h_own == 1)
+    with jax.named_scope("second"):
+        lax.fori_loop(share_at, stage_at, event, 0)
+    with jax.named_scope("early"):
         await_rhs(0)
-
-    with jax.named_scope("early"):
-        @pl.when(outer)
-        def _():
-            by_columns(0, lambda j: j < 0)
-
-    with jax.named_scope("across11"):
-        across(1, 1)
-    with jax.named_scope("across12"):
-        across(1, 2)
+        by_columns(0, lambda j: jnp.logical_not(outer))
+    with jax.named_scope("third"):
+        lax.fori_loop(stage_at, count, event, 0)
+    with jax.named_scope("last"):
         await_rhs(1)
 
-    with jax.named_scope("inner"):
-        @pl.when(jnp.logical_not(outer))
-        def _():
-            by_columns(0, lambda j: j >= 0)
-
-    with jax.named_scope("across13"):
-        across(1, 3)
-    with jax.named_scope("last"):
         @pl.when(outer)
         def _():
             by_columns(1, lambda j: j >= 2)
@@ -364,8 +391,8 @@
             by_rows(1)
 
     with jax.named_scope("settle"):
+        lax.fori_loop(0, 64, sent, 0)
         finish_sends()
-        send_later()
         for row in range(4):
             for part_no in range(2):
                 block = ys.at[2 * (2 * xs(row // 2) + row % 2) + part_no]
@@ -475,7 +502,8 @@
             pltpu.VMEM((7, 5, 16, 128), F32),
             pltpu.VMEM((2, 5, 128, 128), F32),
             pltpu.VMEM((256, 256), F32),
-            dma((128,)), dma((12,)), dma((48,)), dma((64,)), dma((2,)), dma((4,)), dma((4,)),
+            dma((128,)), dma((16,)), dma((4,)), dma((64,)), dma((16,)), dma((64,)), dma((64,)),
+            dma((4,)), dma((4,)),
             dma((16,)), dma((8,)), dma((4, 2)), dma((8,)), dma((2,)), dma((7,)), dma((7,)),
             dma((16,)), dma((7,)), dma((8,)), dma((12,)),
         ],

time: 146 us -> 136 us (0.932)
  Pallas kernels: 142 us -> 132 us
    pallas_call x1, Pallas kernels: 142 us -> 132 us  [local(): pl.pallas_call(kernel, out_shape=(pltpu.VMEM((512, 512), F32), pltpu.VMEM...]
where the time goes in v4:
time: 136 us; the launch traced here: 135 us
  Pallas kernels  132 us (97%)
  local copies, waits for them, and re-layouts  1.94 us (1%)
    pallas_call x1, Pallas kernels, local(): pl.pallas_call(kernel, out_shape=(pltpu.VMEM((512, 512), F32), pltpu.VMEM...  132 us

profile of v4, /device:TPU:15, one launch (start us, length us, event | category | flops | bytes accessed | tf_op | source)
XLA Modules:
  0.0 134.8 jit_solution(12412849164518964267)
XLA Ops:
  0.6 132.2 %shard_map.41 = (f32[512,512]{1,0:T(8,128)S(1)}, f32[512,512]{1,0:T(8,128)S(1)}) custom-call(f32[512,512]{1,0:T(8,128)} %psi.1, f32[512,256]{1,0:T(8,128)} %lower.1), custom_call_target="tpu_custom_call" | custom-call | tf_op jit(solution)/shard_map/pallas_call | solution.py:487
  132.9 1.0 copy.6
  133.8 1.0 copy.7

commit v5 on v4

--- a/solution.py
+++ b/solution.py
@@ -11,26 +11,28 @@
 NG = 8192
 
 EVENTS = (
-    (405115079, 138699458, 461177167, 540649354, 326504717, 695371218, 357657612,
-     602061930, 867409058, 882306733, 1037815163, 1054767524, 4079),
-    (421552280, 154706183, 51775376, 525972442, 295774283, 695256916, 390912688,
-     952720171, 986896625, 668702899, 905070958, 1037987771, 4079),
-    (537428547, 86553697, 676088400, 339051673, 113447715, 128820586, 266742939,
-     476001720, 764594510, 899395293, 800714023, 937152351, 4094),
-    (170143880, 276869381, 122324065, 322081165, 408049898, 246216880, 616932697,
-     850754028, 870431126, 884709167, 519023965, 1054830367, 4093),
-    (9079395, 723717185, 949397769, 300360755, 655282818, 422414764, 988619076,
-     213599477, 102553263, 937150164, 477422973, 402646415, 2014),
-    (697182720, 613714561, 180556139, 43696324, 868932041, 959639056, 114340335,
-     1005134965, 926377492, 256886350, 486106813, 492692827, 4063),
-    (419860520, 52791459, 264574160, 734032607, 605664712, 313058149, 98936670,
-     751313592, 72963852, 871029140, 936856507, 1073471271, 3062),
-    (580917824, 588808450, 705459150, 177333925, 414043185, 455393631, 429554443,
-     347432080, 944193117, 844946351, 1005280531, 1039228406, 4094),
+    (136679875, 88367256, 388871135, 239969290, 544596804, 676684961, 348295964,
+     952036017, 849057963, 600800054, 1073458023, 613899579, 3964),
+    (237002904, 67925577, 437642250, 310163151, 558155168, 950093660, 702887373,
+     368028336, 848214818, 783801468, 617605492, 668401087, 3558),
+    (538452489, 256250307, 388804112, 963021390, 71926099, 590549846, 998967994,
+     527086869, 754079643, 762521917, 666625907, 802581823, 3574),
+    (537667080, 68556361, 102545034, 642103824, 204874921, 495905436, 816641255,
+     511646692, 364008718, 937921398, 1053387991, 886570746, 3964),
+    (10717347, 815241793, 837460516, 281784939, 105193683, 858419335, 1039297388,
+     258269912, 391209332, 1069278532, 439547893, 477061982, 1911),
+    (696945024, 404912321, 615448942, 801390826, 438933826, 129159561, 283077874,
+     457821816, 205861597, 519961909, 233631674, 390055189, 1469),
+    (136679425, 454987992, 643703528, 245146579, 275324003, 102171485, 71915458,
+     954517270, 714271723, 870140254, 770440626, 886565691, 3964),
+    (135798848, 52207886, 596347397, 417641434, 155818331, 278046121, 997576332,
+     729368529, 643724144, 1039219820, 365882541, 903020542, 3574),
 )
-SHARE_AT = (19, 23, 22, 23, 22, 23, 22, 26)
-STAGE_AT = (35, 42, 59, 59, 62, 62, 49, 59)
+SHARE_AT = (12, 14, 33, 34, 37, 37, 17, 19)
+STAGE_AT = (38, 43, 55, 56, 62, 62, 51, 58)
 EVENT_COUNT = (62, 62, 62, 62, 62, 62, 62, 62)
+BY_PAIR = (49678, 526, 32510, 14)
+BOTH_WAYS = (2, 1, 3, 2)
 
 
 def split(a):
@@ -59,7 +61,7 @@
 def kernel(
     psi, lower, out, inter,
     tiles, ys, rhs, owned, part, half, pieces, whole, inverse,
-    tile_sem, ring_sem, back_sem, cross_sem, return_sem, pair_sem, swap_sem, rhs_sem, rhs_send,
+    tile_sem, quarter_send, rhs_sem, rhs_send,
     y_sem, y_send, own_sem, own_send, half_sem, rs_sem, rs_send, ag_sem, ag_send,
     ag_cross, local_sem,
 ):
@@ -79,8 +81,12 @@
     def xs(h):
         return x_low * (1 - h) + (3 - x_low) * h
 
+    low, high = 2 * x_low, 2 * (3 - x_low)
+
     def slot(row, j, a, b):
-        return ((row * 8 + j) * 2 + a) * 2 + b
+        before = jnp.where(row > 0, low + 1, 0) + jnp.where(row > 1, low + 2, 0)
+        before = before + jnp.where(row > 2, high + 1, 0)
+        return ((before + j) * 2 + a) * 2 + b
 
     pending = []
 
@@ -107,8 +113,9 @@
             lower.at[256 * a : 256 * a + 256, :], tiles.at[slot(place, j_own, a, c)],
             local_sem.at[1 + a],
         )
-        load.start()
-        loads.append(load)
+        needed = 2 * j_own + c <= 2 * band + a
+        pl.when(needed)(load.start)
+        loads.append((needed, load))
     psi_here = pltpu.make_async_copy(
         psi.at[:, pl.ds(pl.multiple_of(128 * place, 128), 128)], rhs.at[place], local_sem.at[0]
     )
@@ -130,8 +137,8 @@
     for friend in friends:
         pl.semaphore_signal(barrier, inc=1, device_id=device(*friend), device_id_type=MESH)
     pl.semaphore_wait(barrier, len(friends))
-    for load in loads:
-        load.wait()
+    for needed, load in loads:
+        pl.when(needed)(load.wait)
 
     def quarter(h, a, k, s):
         sgn = 1 - 2 * a
@@ -150,18 +157,22 @@
             out = jnp.logical_and(out, cond)
         return out
 
+    def role(values, h):
+        inner_mask = jnp.where(h == 0, jnp.int32(values[0]), jnp.int32(values[1]))
+        outer_mask = jnp.where(h == 0, jnp.int32(values[2]), jnp.int32(values[3]))
+        return jnp.where(outer, outer_mask, inner_mask)
+
     def by_pair(h, k, s):
-        far = jnp.logical_or(k > 0, s > 0)
-        return jnp.logical_or(
-            both(outer, h == 0, far),
-            both(k == 0, s > 0, jnp.logical_or(h == 1, jnp.logical_not(outer))),
-        )
+        return lax.shift_right_logical(role(BY_PAIR, h), 4 * k + s) % 2 == 1
+
+    def both_ways(h, along_y):
+        return lax.shift_right_logical(role(BOTH_WAYS, h), along_y) % 2 == 1
 
     def copies(h, a, k, s):
         here, real = quarter(h, a, k, s)
         sgn = 1 - 2 * a
         ours = h == h_own
-        short1 = short2 = both(outer, h == 0)
+        short1, short2 = both_ways(h, c), both_ways(h, 1 - c)
         ref = tiles.at[here]
 
         def along(m):
@@ -176,21 +187,22 @@
         last1 = 3 - short1.astype(jnp.int32)
         last2 = 3 - short2.astype(jnp.int32)
         near = both(k == 0, s == 0)
-        line = (h * 4 + k) * 2 + a
-        for cond, sem, target in (
-            (both(real, ours, jnp.logical_or(near, by_pair(h, k, s))),
-             swap_sem.at[line * 4 + s], device(3 - x, y, z, c)),
-            (both(ring(k + 1, 0), s == 0, k < last1),
-             ring_sem.at[line], along(sgn)),
-            (both(ring(3, 0), near, short1), back_sem.at[h * 2 + a], along(-sgn)),
-            (both(ring(k, s + 1), s < last2), cross_sem.at[line * 4 + s], over(sgn)),
-            (both(ring(k, 3), s == 0, short2), return_sem.at[line], over(-sgn)),
-            (real, pair_sem.at[line * 4 + s], device(x, y, z, 1 - c)),
-        ):
-            yield cond, pltpu.make_async_remote_copy(
+        plan = (
+            (both(real, ours, jnp.logical_or(near, by_pair(h, k, s))), device(3 - x, y, z, c)),
+            (both(ring(k + 1, 0), s == 0, k < last1), along(sgn)),
+            (both(ring(3, 0), near, short1), along(-sgn)),
+            (both(ring(k, s + 1), s < last2), over(sgn)),
+            (both(ring(k, 3), s == 0, short2), over(-sgn)),
+            (real, device(x, y, z, 1 - c)),
+        )
+        sem = quarter_send.at[here // 2]
+        return sem, [
+            (cond, pltpu.make_async_remote_copy(
                 src_ref=ref, dst_ref=ref, send_sem=sem, recv_sem=tile_sem.at[here],
                 device_id=target, device_id_type=MESH,
-            )
+            ))
+            for cond, target in plan
+        ]
 
     def finish_sends():
         for cond, copy in pending:
@@ -202,7 +214,7 @@
 
     def own_quarters(ready):
         for a in range(2):
-            for cond, copy in copies(h_own, a, 0, 0):
+            for cond, copy in copies(h_own, a, 0, 0)[1]:
                 pl.when(both(cond, ready(a)))(copy.start)
 
     def decode(code):
@@ -228,13 +240,15 @@
         pl.when(both(real, jnp.logical_not(both(h == h_own, k == 0, s == 0))))(
             lambda: arrived(tiles.at[here], tile_sem.at[here])
         )
-        for cond, copy in copies(h, a, k, s):
+        for cond, copy in copies(h, a, k, s)[1]:
             pl.when(cond)(copy.start)
         return carry
 
     def sent(code, carry):
-        for cond, copy in copies(*decode(code)):
-            pl.when(cond)(copy.wait_send)
+        sem, sends = copies(*decode(code))
+        number = sum(cond.astype(jnp.int32) for cond, _ in sends)
+        for n in range(1, 7):
+            pl.when(number == n)(lambda: arrived(tiles.at[pl.ds(0, n)], sem))
         return carry
 
     own_quarters(lambda a: jnp.logical_not(both(diagonal, c == a)))
@@ -389,19 +403,6 @@
         @pl.when(jnp.logical_not(outer))
         def _():
             by_rows(1)
-
-    with jax.named_scope("settle"):
-        lax.fori_loop(0, 64, sent, 0)
-        finish_sends()
-        for row in range(4):
-            for part_no in range(2):
-                block = ys.at[2 * (2 * xs(row // 2) + row % 2) + part_no]
-                sem = y_send.at[2 * row + part_no]
-                if row < 2:
-                    arrived(block, sem)
-                else:
-                    pl.when(jnp.logical_not(outer))(lambda: arrived(block, sem))
-                pl.when(place != row)(lambda: arrived(block, own_send.at[2 * row + part_no]))
 
     writes = []
     with jax.named_scope("product"):
@@ -449,6 +450,7 @@
             send(None, half.at[:, lines(to)], pieces.at[t - 1],
                  rs_send.at[t - 1], rs_sem.at[t - 1],
                  device(x, 2 * (to % 2) + y_lo, to // 2, c))
+        lax.fori_loop(0, 64, sent, 0)
         total = half[:, lines(m), :]
         for t in range(1, 8):
             arrived(pieces.at[t - 1], rs_sem.at[t - 1])
@@ -463,6 +465,15 @@
             to = lax.rem(m + t, 8)
             share(c, m, ag_send.at[t - 1], device(x, 2 * (to % 2) + y_lo, to // 2, c))
         share(c, m, ag_cross.at[0], device(x, y, z, 1 - c))
+        for row in range(4):
+            for part_no in range(2):
+                block = ys.at[2 * (2 * xs(row // 2) + row % 2) + part_no]
+                sem = y_send.at[2 * row + part_no]
+                if row < 2:
+                    arrived(block, sem)
+                else:
+                    pl.when(jnp.logical_not(outer))(lambda: arrived(block, sem))
+                pl.when(place != row)(lambda: arrived(block, own_send.at[2 * row + part_no]))
         for t in range(1, 8):
             of = lax.rem(m + 8 - t, 8)
             arrived(whole.at[c, :, lines(of)], ag_sem.at[c * 8 + of])
@@ -493,7 +504,7 @@
         in_specs=[pl.BlockSpec(memory_space=pl.ANY)] * 2,
         out_specs=(pl.BlockSpec(memory_space=pltpu.VMEM),) * 2,
         scratch_shapes=[
-            pltpu.VMEM((128, 256, 256), F32),
+            pltpu.VMEM((80, 256, 256), F32),
             pltpu.VMEM((16, 256, 128), F32),
             pltpu.VMEM((4, 512, 128), F32),
             pltpu.VMEM((4, 2, 256, 128), F32),
@@ -502,8 +513,7 @@
             pltpu.VMEM((7, 5, 16, 128), F32),
             pltpu.VMEM((2, 5, 128, 128), F32),
             pltpu.VMEM((256, 256), F32),
-            dma((128,)), dma((16,)), dma((4,)), dma((64,)), dma((16,)), dma((64,)), dma((64,)),
-            dma((4,)), dma((4,)),
+            dma((80,)), dma((40,)), dma((4,)), dma((4,)),
             dma((16,)), dma((8,)), dma((4, 2)), dma((8,)), dma((2,)), dma((7,)), dma((7,)),
             dma((16,)), dma((7,)), dma((8,)), dma((12,)),
         ],

time: 136 us -> 134 us (0.985)
  no operation moved by 1% of the time
where the time goes in v5:
time: 134 us
  Pallas kernels  131 us (98%)
  local copies, waits for them, and re-layouts  1.94 us (1%)
    pallas_call x1, Pallas kernels, local(): pl.pallas_call(kernel, out_shape=(pltpu.VMEM((512, 512), F32), pltpu.VMEM...  131 us

profile of v5, /device:TPU:15, one launch (start us, length us, event | category | flops | bytes accessed | tf_op | source)
XLA Modules:
  0.0 133.7 jit_solution(2802354237097776161)
XLA Ops:
  0.6 131.2 %shard_map.41 = (f32[512,512]{1,0:T(8,128)S(1)}, f32[512,512]{1,0:T(8,128)S(1)}) custom-call(f32[512,512]{1,0:T(8,128)} %psi.1, f32[512,256]{1,0:T(8,128)} %lower.1), custom_call_target="tpu_custom_call" | custom-call | tf_op jit(solution)/shard_map/pallas_call | solution.py:498
  131.8 1.0 copy.6
  132.8 1.0 copy.7

commit v6 on v5

--- a/solution.py
+++ b/solution.py
@@ -11,28 +11,28 @@
 NG = 8192
 
 EVENTS = (
-    (136679875, 88367256, 388871135, 239969290, 544596804, 676684961, 348295964,
-     952036017, 849057963, 600800054, 1073458023, 613899579, 3964),
-    (237002904, 67925577, 437642250, 310163151, 558155168, 950093660, 702887373,
-     368028336, 848214818, 783801468, 617605492, 668401087, 3558),
-    (538452489, 256250307, 388804112, 963021390, 71926099, 590549846, 998967994,
-     527086869, 754079643, 762521917, 666625907, 802581823, 3574),
-    (537667080, 68556361, 102545034, 642103824, 204874921, 495905436, 816641255,
-     511646692, 364008718, 937921398, 1053387991, 886570746, 3964),
-    (10717347, 815241793, 837460516, 281784939, 105193683, 858419335, 1039297388,
-     258269912, 391209332, 1069278532, 439547893, 477061982, 1911),
-    (696945024, 404912321, 615448942, 801390826, 438933826, 129159561, 283077874,
-     457821816, 205861597, 519961909, 233631674, 390055189, 1469),
-    (136679425, 454987992, 643703528, 245146579, 275324003, 102171485, 71915458,
-     954517270, 714271723, 870140254, 770440626, 886565691, 3964),
-    (135798848, 52207886, 596347397, 417641434, 155818331, 278046121, 997576332,
-     729368529, 643724144, 1039219820, 365882541, 903020542, 3574),
+    (157557187, 88368648, 457242079, 239904395, 561644356, 676684957, 475208745,
+     582921100, 966683384, 600800050, 1073458605, 613899579, 3964),
+    (117981848, 421847558, 437016464, 310163151, 558155168, 232879964, 346201683,
+     576170672, 848280300, 1050139772, 1066617715, 668401070, 3558),
+    (538452489, 256250307, 388804112, 963021390, 373915987, 833331981, 998967492,
+     447608085, 1016458395, 762466156, 1067378547, 1052727732, 3574),
+    (50890272, 68556361, 102545034, 642103824, 204874921, 495832100, 666547155,
+     830008298, 364008735, 937921398, 854158551, 1037262590, 4092),
+    (10717347, 815241793, 837460516, 61673161, 843412678, 172650631, 1039321523,
+     423285464, 773014927, 892858335, 439375125, 477063087, 1911),
+    (637704360, 404912321, 616583406, 46076202, 174765669, 270039881, 971205874,
+     455919452, 290421522, 528219445, 339460026, 401695573, 3919),
+    (157548611, 678196744, 324966539, 591032998, 812194895, 36980550, 524363077,
+     954517270, 514517743, 865160677, 771714738, 886565691, 3964),
+    (135794816, 51671310, 589966888, 417641434, 304453979, 207262756, 300801706,
+     508614620, 761166891, 1011817254, 365882557, 901730302, 3574),
 )
-SHARE_AT = (12, 14, 33, 34, 37, 37, 17, 19)
-STAGE_AT = (38, 43, 55, 56, 62, 62, 51, 58)
+SHARE_AT = (14, 13, 42, 41, 43, 46, 15, 19)
+STAGE_AT = (38, 42, 52, 56, 62, 62, 51, 62)
 EVENT_COUNT = (62, 62, 62, 62, 62, 62, 62, 62)
-BY_PAIR = (49678, 526, 32510, 14)
-BOTH_WAYS = (2, 1, 3, 2)
+BY_PAIR = ((51726, 51726), (526, 526), (32510, 32510), (14, 14))
+BOTH_WAYS = ((2, 2), (1, 1), (3, 3), (2, 2))
 
 
 def split(a):
@@ -40,14 +40,26 @@
     return high, (a - high.astype(F32)).astype(BF16)
 
 
-def product(a, b, dims=(((1,), (0,)), ((), ()))):
+def product(a, b):
     ah, al = split(a)
     bh, bl = split(b)
 
     def dot(p, q):
-        return lax.dot_general(p, q, dims, preferred_element_type=F32)
+        return jnp.dot(p, q, preferred_element_type=F32)
 
     return dot(ah, bh) + (dot(ah, bl) + dot(al, bh))
+
+
+def outer_product(a, b):
+    ah, al = split(a)
+    bh, bl = split(b)
+
+    def dot(p, q):
+        return lax.dot_general(p, q, (((1,), (1,)), ((), ())), preferred_element_type=F32)
+
+    return dot(ah, bl) + dot(
+        jnp.concatenate([ah, al], axis=1), jnp.concatenate([bh, bh], axis=1)
+    )
 
 
 def narrow_product(a, b):
@@ -158,9 +170,10 @@
         return out
 
     def role(values, h):
-        inner_mask = jnp.where(h == 0, jnp.int32(values[0]), jnp.int32(values[1]))
-        outer_mask = jnp.where(h == 0, jnp.int32(values[2]), jnp.int32(values[3]))
-        return jnp.where(outer, outer_mask, inner_mask)
+        of = [jnp.where(c == 0, jnp.int32(a), jnp.int32(b)) for a, b in values]
+        return jnp.where(
+            outer, jnp.where(h == 0, of[2], of[3]), jnp.where(h == 0, of[0], of[1])
+        )
 
     def by_pair(h, k, s):
         return lax.shift_right_logical(role(BY_PAIR, h), 4 * k + s) % 2 == 1
@@ -425,9 +438,8 @@
             block = owned[q].reshape(512, 128)
             at = 0
             for r in range(4):
-                term = product(
-                    block[128 * r : 128 * r + 128], block[: 128 * r + 128],
-                    (((1,), (1,)), ((), ())),
+                term = outer_product(
+                    block[128 * r : 128 * r + 128], block[: 128 * r + 128]
                 )
                 for s in range(r + 1):
                     here = term[:, 128 * s : 128 * s + 128]

time: 134 us -> 130 us (0.970)
  Pallas kernels: 131 us -> 128 us
    pallas_call x1, Pallas kernels: 131 us -> 128 us  [local(): pl.pallas_call(kernel, out_shape=(pltpu.VMEM((512, 512), F32), pltpu.VMEM...]
where the time goes in v6:
time: 130 us
  Pallas kernels  128 us (98%)
  local copies, waits for them, and re-layouts  1.94 us (1%)
    pallas_call x1, Pallas kernels, local(): pl.pallas_call(kernel, out_shape=(pltpu.VMEM((512, 512), F32), pltpu.VMEM...  128 us

profile of v6, /device:TPU:15, one launch (start us, length us, event | category | flops | bytes accessed | tf_op | source)
XLA Modules:
  0.0 130.2 jit_solution(16833832647987864280)
XLA Ops:
  0.6 127.6 %shard_map.41 = (f32[512,512]{1,0:T(8,128)S(1)}, f32[512,512]{1,0:T(8,128)S(1)}) custom-call(f32[512,512]{1,0:T(8,128)} %psi.1, f32[512,256]{1,0:T(8,128)} %lower.1), custom_call_target="tpu_custom_call" | custom-call | tf_op jit(solution)/shard_map/pallas_call | solution.py:510
  128.3 1.0 copy.6
  129.2 1.0 copy.7

commit v7 on v6

--- a/solution.py
+++ b/solution.py
@@ -11,25 +11,25 @@
 NG = 8192
 
 EVENTS = (
-    (157557187, 88368648, 457242079, 239904395, 561644356, 676684957, 475208745,
-     582921100, 966683384, 600800050, 1073458605, 613899579, 3964),
-    (117981848, 421847558, 437016464, 310163151, 558155168, 232879964, 346201683,
-     576170672, 848280300, 1050139772, 1066617715, 668401070, 3558),
-    (538452489, 256250307, 388804112, 963021390, 373915987, 833331981, 998967492,
-     447608085, 1016458395, 762466156, 1067378547, 1052727732, 3574),
-    (50890272, 68556361, 102545034, 642103824, 204874921, 495832100, 666547155,
-     830008298, 364008735, 937921398, 854158551, 1037262590, 4092),
-    (10717347, 815241793, 837460516, 61673161, 843412678, 172650631, 1039321523,
-     423285464, 773014927, 892858335, 439375125, 477063087, 1911),
-    (637704360, 404912321, 616583406, 46076202, 174765669, 270039881, 971205874,
-     455919452, 290421522, 528219445, 339460026, 401695573, 3919),
-    (157548611, 678196744, 324966539, 591032998, 812194895, 36980550, 524363077,
-     954517270, 514517743, 865160677, 771714738, 886565691, 3964),
-    (135794816, 51671310, 589966888, 417641434, 304453979, 207262756, 300801706,
-     508614620, 761166891, 1011817254, 365882557, 901730302, 3574),
+    (35402841, 403997254, 191693791, 239968919, 511824708, 362898593, 834718300,
+     948628116, 849059307, 663669747, 1072426413, 1016552763, 2365),
+    (102506776, 174338574, 438589328, 523088850, 558155168, 685864796, 816289043,
+     576168810, 602917612, 634379185, 1066659122, 664493037, 3511),
+    (538452489, 273027523, 675118633, 962912907, 206143827, 602649430, 806557866,
+     447608085, 1016481691, 768200556, 668198771, 802581439, 3511),
+    (56754690, 68556361, 102539994, 642103824, 227093068, 328117276, 666520271,
+     836365277, 626060117, 931110444, 845129139, 886570750, 3901),
+    (31598824, 143658601, 720046449, 101519049, 35595371, 754398439, 1012818578,
+     255513304, 336698646, 1062600622, 439375797, 930308975, 1883),
+    (25848384, 86145256, 814758808, 78270635, 182033393, 152857754, 313854771,
+     493735544, 215293387, 1073431443, 351250398, 1012495189, 1021),
+    (392429635, 463831561, 322577128, 597469575, 488182769, 96596804, 380458138,
+     791909378, 514516792, 848509268, 1052209146, 1039096631, 3388),
+    (135798785, 940339470, 589965829, 304936633, 270947928, 464045481, 474339643,
+     339113978, 398584235, 1011817261, 365882557, 920080382, 3063),
 )
-SHARE_AT = (14, 13, 42, 41, 43, 46, 15, 19)
-STAGE_AT = (38, 42, 52, 56, 62, 62, 51, 62)
+SHARE_AT = (13, 13, 41, 34, 35, 44, 15, 15)
+STAGE_AT = (38, 42, 52, 56, 62, 62, 51, 61)
 EVENT_COUNT = (62, 62, 62, 62, 62, 62, 62, 62)
 BY_PAIR = ((51726, 51726), (526, 526), (32510, 32510), (14, 14))
 BOTH_WAYS = ((2, 2), (1, 1), (3, 3), (2, 2))

time: 130 us -> 129 us (level)
  Pallas kernels: 128 us -> 126 us
where the time goes in v7:
time: 129 us
  Pallas kernels  126 us (98%)
  local copies, waits for them, and re-layouts  1.94 us (2%)
    pallas_call x1, Pallas kernels, local(): pl.pallas_call(kernel, out_shape=(pltpu.VMEM((512, 512), F32), pltpu.VMEM...  126 us

profile of v7, /device:TPU:15, one launch (start us, length us, event | category | flops | bytes accessed | tf_op | source)
XLA Modules:
  0.0 128.9 jit_solution(12738029097585258270)
XLA Ops:
  0.6 126.3 %shard_map.41 = (f32[512,512]{1,0:T(8,128)S(1)}, f32[512,512]{1,0:T(8,128)S(1)}) custom-call(f32[512,512]{1,0:T(8,128)} %psi.1, f32[512,256]{1,0:T(8,128)} %lower.1), custom_call_target="tpu_custom_call" | custom-call | tf_op jit(solution)/shard_map/pallas_call | solution.py:510
  127.0 1.0 copy.6
  127.9 1.0 copy.7

commit v8 on v7

--- a/solution.py
+++ b/solution.py
@@ -463,6 +463,9 @@
                  rs_send.at[t - 1], rs_sem.at[t - 1],
                  device(x, 2 * (to % 2) + y_lo, to // 2, c))
         lax.fori_loop(0, 64, sent, 0)
+        finish_sends()
+        for write in writes:
+            write.wait()
         total = half[:, lines(m), :]
         for t in range(1, 8):
             arrived(pieces.at[t - 1], rs_sem.at[t - 1])
@@ -501,8 +504,6 @@
                     inter[128 * s : 128 * s + 128, 128 * r : 128 * r + 128] = block.T
                 at += 1
     finish_sends()
-    for write in writes:
-        write.wait()
 
 
 def local(psi, lower):

time: 129 us -> 129 us (level)
  no operation moved by 1% of the time
where the time goes in v8:
time: 129 us
  Pallas kernels  126 us (98%)
  local copies, waits for them, and re-layouts  1.94 us (2%)
    pallas_call x1, Pallas kernels, local(): pl.pallas_call(kernel, out_shape=(pltpu.VMEM((512, 512), F32), pltpu.VMEM...  126 us

profile of v8, /device:TPU:15, one launch (start us, length us, event | category | flops | bytes accessed | tf_op | source)
XLA Modules:
  0.0 128.9 jit_solution(8396788452464425694)
XLA Ops:
  0.6 126.3 %shard_map.41 = (f32[512,512]{1,0:T(8,128)S(1)}, f32[512,512]{1,0:T(8,128)S(1)}) custom-call(f32[512,512]{1,0:T(8,128)} %psi.1, f32[512,256]{1,0:T(8,128)} %lower.1), custom_call_target="tpu_custom_call" | custom-call | tf_op jit(solution)/shard_map/pallas_call | solution.py:511
  126.9 1.0 copy.6
  127.9 1.0 copy.7
